TPU v7x, 32 devices: a whole 2x2x4 slice. The times are simulated.
32 devices in a mesh: group: 2 (over y), win: 16 (over z, x, core).
Axes of the slice: x: 2, y: 2, z: 4, core: 2. Of those that a mesh axis runs over, the one named last changes fastest.
Arguments:
- img_qkv: bfloat16 [64, 256, 4608], P(('group', 'win')), parts along dimension 0, may hold values from -100 to 100
- txt_kv: bfloat16 [64, 128, 3072], P(('group', 'win')), parts along dimension 0, may hold values from -6 to 6
- hidden: bfloat16 [64, 256, 3072], P(('group', 'win')), parts along dimension 0, may hold values from -6 to 6
- w_proj: bfloat16 [1536, 3072], P('win'), may hold values from -0.15625 to 0.15625
- w_out: bfloat16 [3072, 64], replicated, may hold values from -0.109375 to 0.109375
- modulation: float32 [6, 3072], P('group'), parts along dimension 0, may hold values from -3 to 3
- anchors: int32 [64, 2], P(('group', 'win')), parts along dimension 0, may hold values from 0 to 255, as said below
- blend_weight: int32 [64, 32, 32], P(('group', 'win')), parts along dimension 0, may hold values from 0 to 8
Outputs:
- velocity: float32 [16, 512, 64], P(None, ('group', 'win')), parts along dimension 1
There are 2 independent parts, one for each index of `group`. A program takes and returns all parts, laid end to end along the dimension named above; an argument that names none is the same for every part. Nothing has to cross between parts.
Inputs may be any that keep to these rules, and one draw needn't show every extreme that they name: `anchors`: window w's anchor row lies in [16 * (w // 2), 16 * (w // 2) + 16); its columns wrap around the panorama; the 2 windows w with the same w // 2 have anchor columns (s + 32 * (w % 2)) mod 64 for one s of that band, so that they cover all 64 columns.
All inputs are finite; a program needn't handle non-finite values.
Results may differ from a plain program's by a relative error of at most 0.0029.
Values may be sent and summed in bfloat16 or wider, within the bound.
A program may use at most 128 MiB of HBM per device.

v0:
```python
import functools
import math

import jax
import jax.numpy as jnp
from jax import lax
from jax.experimental import pallas as pl
from jax.experimental.pallas import tpu as pltpu
from jax.sharding import PartitionSpec as P

HD = 128
C = 16
HEADS = 12
PATCH = 2
WIN = 32
LW = 64
BAND = 16
GRID = 16


def shifted(block, axis, distance):
    devices = range(lax.axis_size(axis))
    route = [(i - distance, i) for i in devices if i - distance in devices]
    return lax.ppermute(block, axis, route)


def place_window(canvas, totals, contrib, weights, row_at, col_at):
    zero_index = jnp.zeros((), jnp.int32)
    region = lax.dynamic_slice(canvas, (zero_index, row_at, col_at), (C, WIN, WIN))
    canvas = lax.dynamic_update_slice(canvas, region + contrib, (zero_index, row_at, col_at))
    weight_region = lax.dynamic_slice(totals, (row_at, col_at), (WIN, WIN))
    totals = lax.dynamic_update_slice(totals, weight_region + weights, (row_at, col_at))
    return (canvas, totals)


def fold_columns(field):
    span_cols = field.shape[-1] - WIN
    leading = field[..., :span_cols]
    wrapped = field[..., span_cols:]
    padding = [(0, 0)] * (field.ndim - 1) + [(0, span_cols - WIN)]
    return leading + jnp.pad(wrapped, padding)


def plain_shards(img_qkv, txt_kv, hidden, w_proj, w_out, modulation, anchors, blend_weight):
    window_count, tokens, _ = img_qkv.shape
    features = HEADS * HD
    queries = img_qkv[:, :, :features].reshape(window_count, tokens, HEADS, HD)
    all_keys = jnp.concatenate(
        [txt_kv[:, :, :features], img_qkv[:, :, features : 2 * features]], axis=1
    )
    all_keys = all_keys.reshape(window_count, -1, HEADS, HD)
    all_values = jnp.concatenate([txt_kv[:, :, features:], img_qkv[:, :, 2 * features :]], axis=1)
    all_values = all_values.reshape(window_count, -1, HEADS, HD)
    scores = jnp.einsum(
        "wqhd,wkhd->whqk", queries, all_keys, preferred_element_type=jnp.float32
    ) / math.sqrt(HD)
    scores = scores - jnp.max(scores, axis=-1, keepdims=True)
    exp_scores = jnp.exp(scores)
    soft_weights = (exp_scores / jnp.sum(exp_scores, axis=-1, keepdims=True)).astype(jnp.bfloat16)
    attended = jnp.einsum(
        "whqk,wkhd->wqhd", soft_weights, all_values, preferred_element_type=jnp.float32
    )
    attended = attended.reshape(window_count * tokens, features).astype(jnp.bfloat16)
    whole_proj = lax.all_gather(w_proj, "win", axis=0, tiled=True)
    projected = jnp.dot(attended, whole_proj, preferred_element_type=jnp.float32)
    residual = (
        hidden.reshape(window_count * tokens, -1).astype(jnp.float32) + modulation[0] * projected
    )
    row_mean = jnp.mean(residual, axis=-1, keepdims=True)
    centred = residual - row_mean
    row_var = jnp.mean(centred * centred, axis=-1, keepdims=True)
    normed = centred * lax.rsqrt(row_var + 1e-06)
    modulated = (normed * (1.0 + modulation[1]) + modulation[2]).astype(jnp.bfloat16)
    patch_vel = jnp.dot(modulated, w_out, preferred_element_type=jnp.float32)
    patch_grid = patch_vel.reshape(window_count, GRID, GRID, C, PATCH, PATCH)
    window_vel = patch_grid.transpose(0, 3, 1, 4, 2, 5).reshape(window_count, C, WIN, WIN)
    weights = blend_weight.astype(jnp.float32)
    contrib = window_vel * weights[:, None]
    band_start = lax.axis_index("win") * BAND
    canvas = jnp.zeros((C, BAND + WIN, LW + WIN), jnp.float32)
    totals = jnp.zeros((BAND + WIN, LW + WIN), jnp.float32)

    def add_one(window, running):
        row_at = anchors[window, 0] - band_start
        col_at = anchors[window, 1]
        return place_window(
            running[0], running[1], contrib[window], weights[window], row_at, col_at
        )

    canvas, totals = lax.fori_loop(0, window_count, add_one, (canvas, totals))
    canvas = fold_columns(canvas)
    totals = fold_columns(totals)
    own_canvas = canvas[:, :BAND]
    own_totals = totals[:BAND]
    near_canvas = canvas[:, BAND : 2 * BAND]
    near_totals = totals[BAND : 2 * BAND]
    far_canvas = canvas[:, 2 * BAND :]
    far_totals = totals[2 * BAND :]
    prev_canvas, prev_totals = shifted((near_canvas, near_totals), "win", 1)
    second_canvas, second_totals = shifted((far_canvas, far_totals), "win", 2)
    sum_canvas = own_canvas + prev_canvas + second_canvas
    sum_totals = own_totals + prev_totals + second_totals
    return sum_canvas / jnp.maximum(sum_totals, 1.0)[None]


LOG2E = 1.4426950408889634
MESH_ID = pl.DeviceIdType.MESH


def block_kernel(
    n,
    qkv_hbm,
    txt_hbm,
    hid_hbm,
    wp_hbm,
    wout_ref,
    mod_ref,
    out_ref,
    qkv,
    txt,
    hid,
    weights,
    att,
    lhs,
    acc,
    load_sems,
    cw_send,
    cw_recv,
    ccw_send,
    ccw_recv,
    y_send,
    y_recv,
    own_sems,
    part_send,
    part_recv,
):
    windows, tokens, _ = qkv.shape
    text = txt.shape[1]
    rows = wp_hbm.shape[0]
    width = weights.shape[1]
    features = HEADS * HD
    third = width // 3
    half = third // 2
    chips = n // 2
    length = chips // 2
    group = lax.axis_index("group")
    me = lax.axis_index("win")
    core = me % 2
    chip = me // 2
    depth, side = chip // 2, chip % 2
    place = depth + side * (chips - 1 - 2 * depth)

    def chip_at(position):
        spot = (position + chips) % chips
        turn = spot // length
        return 2 * (spot + turn * (chips - 1 - 2 * spot)) + turn

    def ranked(which_chip, which_core):
        return which_chip * 2 + which_core

    onward = (group, ranked(chip_at(place + 1), core))
    backward = (group, ranked(chip_at(place - 1), core))
    across = (1 - group, me)
    partner = (group, me + 1 - 2 * core)
    own_third = group * (2 * third)
    far_third = (1 - group) * (2 * third)

    def region(which_chip, which_core, col, cols):
        row = pl.multiple_of(ranked(which_chip, which_core) * rows, 16)
        return weights.at[pl.ds(row, rows), pl.ds(pl.multiple_of(col, 128), cols)]

    def remote(ref, send, recv, device):
        return pltpu.make_async_remote_copy(
            src_ref=ref, dst_ref=ref, send_sem=send, recv_sem=recv,
            device_id=device, device_id_type=MESH_ID,
        )

    def cw(step, sub, hop):
        ref = region(chip_at(place - step - hop), core, own_third + sub * half, half)
        return remote(ref, cw_send.at[step, sub], cw_recv.at[step, sub], onward)

    def ccw(step, sub, hop):
        ref = region(chip_at(place + step + hop), core, third + sub * half, half)
        return remote(ref, ccw_send.at[step, sub], ccw_recv.at[step, sub], backward)

    def yy(step, sub, col):
        ref = region(chip_at(place - step - 1), core, col + sub * half, half)
        return remote(ref, y_send.at[step, sub], y_recv.at[step, sub], across)

    def part(step, kind, which_core):
        col = (own_third, third, far_third)[kind]
        source = chip_at(place + step + 1) if kind == 1 else chip_at(place - step - 1)
        ref = region(source, which_core, col, third)
        return remote(ref, part_send.at[step, kind], part_recv.at[step, kind], partner)

    def part_own(which_core):
        ref = region(chip, which_core, 0, width)
        return remote(ref, own_sems.at[0], own_sems.at[1], partner)

    own_load = pltpu.make_async_copy(wp_hbm, region(chip, core, 0, width), load_sems.at[0])
    own_load.start()
    loads = []
    for w in range(windows):
        loads.append(
            (
                pltpu.make_async_copy(qkv_hbm.at[w], qkv.at[w], load_sems.at[1 + 2 * w]),
                pltpu.make_async_copy(txt_hbm.at[w], txt.at[w], load_sems.at[2 + 2 * w]),
            )
        )
    hid_load = pltpu.make_async_copy(hid_hbm, hid, load_sems.at[1 + 2 * windows])

    barrier = pltpu.get_barrier_semaphore()
    for device in (onward, backward, across, partner):
        pl.semaphore_signal(barrier, inc=1, device_id=device, device_id_type=MESH_ID)
    pl.semaphore_wait(barrier, 4)

    own_load.wait()
    for sub in range(2):
        cw(0, sub, 0).start()
        ccw(0, sub, 0).start()
    part_own(core).start()
    for pair in loads:
        for copy in pair:
            copy.start()
    hid_load.start()

    scale = LOG2E / math.sqrt(HD)

    def attend(w, h):
        col = pl.multiple_of(h * HD, HD)
        cols = pl.ds(col, HD)
        kcols = pl.ds(pl.multiple_of(col + features, HD), HD)
        vcols = pl.ds(pl.multiple_of(col + 2 * features, HD), HD)
        q = qkv[w, :, cols]
        dims = (((1,), (1,)), ((), ()))
        st = lax.dot_general(txt[w, :, cols], q, dims, preferred_element_type=jnp.float32)
        si = lax.dot_general(qkv[w, :, kcols], q, dims, preferred_element_type=jnp.float32)
        top = jnp.maximum(jnp.max(st, axis=0, keepdims=True), jnp.max(si, axis=0, keepdims=True))
        pt = jnp.exp2((st - top) * scale)
        pi = jnp.exp2((si - top) * scale)
        total = jnp.sum(pt, axis=0, keepdims=True) + jnp.sum(pi, axis=0, keepdims=True)
        back = (((0,), (0,)), ((), ()))
        out = lax.dot_general(
            txt[w, :, kcols], pt.astype(jnp.bfloat16), back, preferred_element_type=jnp.float32
        ) + lax.dot_general(
            qkv[w, :, vcols], pi.astype(jnp.bfloat16), back, preferred_element_type=jnp.float32
        )
        att[pl.ds(col, HD), pl.ds(pl.multiple_of(w * tokens, 128), tokens)] = (
            out * (1.0 / total)
        ).astype(jnp.bfloat16)

    tile = 512 if third % 512 == 0 else third

    def project(held, col, first=False):
        spots = [pl.ds(pl.multiple_of(q * (2 * rows), 16), 2 * rows) for q in held]
        deep = 2 * rows * len(held)
        lhs[:, :deep] = jnp.concatenate([att[spot, :] for spot in spots], axis=0).T

        def one(t, carry):
            at = pl.ds(pl.multiple_of(col + t * tile, 128), tile)
            rhs = jnp.concatenate([weights[spot, at] for spot in spots], axis=0)
            term = jnp.dot(lhs[:, :deep], rhs, preferred_element_type=jnp.float32)
            acc[:, at] = term if first else acc[:, at] + term
            return carry

        lax.fori_loop(0, third // tile, one, 0)

    def project_kind(group_steps, kind, with_own=False):
        for step in group_steps:
            part(step, kind, 1 - core).wait_recv()
        sign = 1 if kind == 1 else -1
        held = [chip_at(place + sign * (step + 1)) for step in group_steps]
        if with_own:
            held = [chip] + held
        project(held, (own_third, third, far_third)[kind], first=with_own)

    def serve(step, sub, more):
        cw(step, sub, 1).wait_recv()
        if more:
            cw(step + 1, sub, 0).start()
        yy(step, sub, own_third).start()
        ccw(step, sub, 1).wait_recv()
        if more:
            ccw(step + 1, sub, 0).start()

    def hand_over(step):
        part(step, 0, core).start()
        part(step, 1, core).start()

    def hand_across(step):
        for sub in range(2):
            yy(step, sub, far_third).wait_recv()
        part(step, 2, core).start()

    steps = chips - 1
    early = (steps + 1) // 2
    slots = 2 * early
    units = windows * HEADS
    per = -(-units // slots)
    done = 0
    plan = []
    for slot in range(slots):
        plan.append(range(done, min(units, done + per)))
        done = min(units, done + per)
    ready = set()
    for step in range(early):
        for sub in range(2):
            for unit in plan[2 * step + sub]:
                w, h = unit // HEADS, unit % HEADS
                if w not in ready:
                    for copy in loads[w]:
                        copy.wait()
                    ready.add(w)
                attend(w, h)
            serve(step, sub, step + 1 < steps)
        hand_over(step)
        if step >= 1:
            hand_across(step - 1)
    part_own(1 - core).wait_recv()
    opening = list(range(early - 1))
    middle = list(range(early - 1, steps - 2))
    closing = list(range(max(steps - 2, early - 1), steps))
    work = [(opening, kind, True) for kind in (0, 2, 1)]
    work += [None] * (2 * (steps - early) - 5)
    if middle:
        work += [(middle, kind, False) for kind in (0, 2, 1)]
    for step in range(early, steps):
        for sub in range(2):
            quota = 1 if step < steps - 1 else 2
            for _ in range(quota):
                if work:
                    piece = work.pop(0)
                    if piece is not None:
                        project_kind(*piece)
            serve(step, sub, step + 1 < steps)
        hand_over(step)
        hand_across(step - 1)
    for piece in work:
        if piece is not None:
            project_kind(*piece)
    for step in closing[:-1]:
        for kind in range(3):
            project_kind([step], kind)
    hand_across(steps - 1)
    for kind in (0, 1, 2):
        project_kind(closing[-1:], kind)

    hid_load.wait()
    block = 256 if acc.shape[0] % 256 == 0 else acc.shape[0]
    gate = mod_ref[0:1, :]
    gain = 1.0 + mod_ref[1:2, :]
    shift = mod_ref[2:3, :]

    def norm(b, carry):
        at = pl.ds(pl.multiple_of(b * block, 16), block)
        residual = hid[at, :].astype(jnp.float32) + gate * acc[at, :]
        mean = jnp.sum(residual, axis=-1, keepdims=True) * (1.0 / width)
        centred = residual - mean
        var = jnp.sum(centred * centred, axis=-1, keepdims=True) * (1.0 / width)
        modulated = (centred * lax.rsqrt(var + 1e-06) * gain + shift).astype(jnp.bfloat16)
        out_ref[:, pl.ds(pl.multiple_of(b * block, 128), block)] = lax.dot_general(
            wout_ref[...], modulated, (((1,), (1,)), ((), ())), preferred_element_type=jnp.float32
        )
        return carry

    lax.fori_loop(0, acc.shape[0] // block, norm, 0)

    for step in range(steps):
        for sub in range(2):
            cw(step, sub, 0).wait_send()
            ccw(step, sub, 0).wait_send()
            yy(step, sub, own_third).wait_send()
        for kind in range(3):
            part(step, kind, core).wait_send()
    part_own(core).wait_send()


def shards(n, img_qkv, txt_kv, hidden, w_proj, w_out, modulation, anchors, blend_weight):
    windows, tokens, qkv_width = img_qkv.shape
    rows, width = w_proj.shape
    total = windows * tokens
    steps = n // 2 - 1
    any_space = pl.BlockSpec(memory_space=pl.ANY)
    vmem = pl.BlockSpec(memory_space=pltpu.VMEM)
    dma = pltpu.SemaphoreType.DMA
    patch_vel = pl.pallas_call(
        functools.partial(block_kernel, n),
        out_shape=jax.ShapeDtypeStruct((w_out.shape[1], total), jnp.float32),
        in_specs=[any_space] * 4 + [vmem] * 2,
        out_specs=vmem,
        scratch_shapes=[
            pltpu.VMEM(img_qkv.shape, jnp.bfloat16),
            pltpu.VMEM(txt_kv.shape, jnp.bfloat16),
            pltpu.VMEM((total, width), jnp.bfloat16),
            pltpu.VMEM((n * rows, width), jnp.bfloat16),
            pltpu.VMEM((n * rows, total), jnp.bfloat16),
            pltpu.VMEM((total, 2 * rows * (n // 4)), jnp.bfloat16),
            pltpu.VMEM((total, width), jnp.float32),
            dma((2 + 2 * windows,)),
            dma((steps, 2)),
            dma((steps, 2)),
            dma((steps, 2)),
            dma((steps, 2)),
            dma((steps, 2)),
            dma((steps, 2)),
            dma((2,)),
            dma((steps, 3)),
            dma((steps, 3)),
        ],
        compiler_params=pltpu.CompilerParams(
            collective_id=0, has_side_effects=True, vmem_limit_bytes=60 * 1024 * 1024
        ),
    )(img_qkv, txt_kv, hidden.reshape(total, width), w_proj, w_out.T, modulation)

    weights = blend_weight.astype(jnp.float32)
    grid = patch_vel.reshape(C, PATCH, PATCH, windows, GRID, GRID)
    window_vel = grid.transpose(3, 0, 4, 1, 5, 2).reshape(windows, C, WIN, WIN)
    contrib = jnp.concatenate([window_vel * weights[:, None], weights[:, None]], axis=1)
    band_start = lax.axis_index("win") * BAND
    cells = jnp.arange(WIN, dtype=jnp.int32)
    row_of = anchors[:, 0:1] - band_start + cells
    col_of = (anchors[:, 1:2] + cells) % LW
    row_hot = (row_of[:, :, None] == jnp.arange(BAND + WIN, dtype=jnp.int32)).astype(jnp.float32)
    col_hot = (col_of[:, :, None] == jnp.arange(LW, dtype=jnp.int32)).astype(jnp.float32)
    wide = jnp.einsum("wcab,wbs->wcas", contrib, col_hot, precision=lax.Precision.HIGHEST)
    canvas = jnp.einsum("wcas,war->crs", wide, row_hot, precision=lax.Precision.HIGHEST)
    near = shifted(canvas[:, BAND : 2 * BAND], "win", 1)
    far = shifted(canvas[:, 2 * BAND :], "win", 2)
    summed = canvas[:, :BAND] + near + far
    return summed[:C] / jnp.maximum(summed[C], 1.0)[None]


def solution(mesh):
    in_specs = (
        P(("group", "win"), None, None),
        P(("group", "win"), None, None),
        P(("group", "win"), None, None),
        P("win", None),
        P(),
        P("group", None),
        P(("group", "win"), None),
        P(("group", "win"), None, None),
    )
    out_specs = P(None, ("group", "win"), None)
    n = mesh.shape["win"]

    def body(*args):
        rows, width = args[3].shape
        ringed = mesh.shape["group"] == 2 and n % 4 == 0 and rows % 16 == 0 and width % 768 == 0
        if ringed:
            return shards(n, *args)
        return plain_shards(*args)

    return jax.shard_map(body, mesh=mesh, in_specs=in_specs, out_specs=out_specs, check_vma=False)
```

profile of v0, /device:TPU:8, one launch (start us, length us, event | category | flops | bytes accessed | tf_op | source)
XLA Modules:
  0.0 64.1 jit_solution(7487268100928794369)
XLA Ops:
  0.0 0.8 %fusion.15 = (f32[2,32,32]{2,1,0:T(8,128)S(1)}, f32[2,1,32,32]{3,2,0,1:T(8,128)S(1)}) fusion(s32[2,32,32]{2,1,0:T(8,128)} %param.15), kind=kLoop, calls=%fused_computation.27 | loop fusion | flops 2048 | bytes 24576 | tf_op jit(solution)/shard_map/convert_element_type | solution.py:415
  0.8 48.8 %shard_map.82 = f32[64,512]{1,0:T(8,128)} custom-call(bf16[2,256,4608]{2,1,0:T(8,128)(2,1)} %qkv_hbm.1, bf16[2,128,3072]{2,1,0:T(8,128)(2,1)} %txt_hbm.1, bf16[512,3072]{1,0:T(8,128)(2,1)} %bitcast.22, bf16[96,3072]{1,0:T(8,128)(2,1)} %wp_hbm.1, bf16[64,3072]{1,0:T(8,128)(2,1)} %bitcast.23, f32[3,3072]{1,0:T(4,128)} %mod_ref.1), custom_call_target="tpu_custom_call" | custom-call | tf_op jit(solution)/shard_map/pallas_call | solution.py:386
  49.5 0.0 copy-start
  49.6 1.3 %reshape.66 = f32[16,2,2,2,16,16]{5,4,3,2,1,0:T(8,128)S(1)} reshape(f32[64,512]{1,0:T(8,128)} %shard_map.82) | data formatting | bytes 262144 | tf_op jit(solution)/shard_map/reshape | solution.py:416
  50.8 0.8 %copy.11 = f32[16,2,2,2,16,16]{0,2,5,1,4,3:T(2,128)S(1)} copy(f32[16,2,2,2,16,16]{5,4,3,2,1,0:T(8,128)S(1)} %reshape.66) | data formatting | bytes 262144 | tf_op jit(solution)/shard_map/reshape | solution.py:416
  51.6 0.5 copy.12
  52.2 0.0 copy-done
  52.2 0.2 subtract_reduce_fusion
  52.4 0.1 and_select_fusion
  52.4 0.4 fusion
  52.9 0.4 convolution_bitcast_fusion
  53.4 2.6 %collective-permute-start.1 = (f32[17,16,64]{2,1,0:T(8,128)S(1)}, f32[17,16,64]{2,1,0:T(8,128)S(1)}, u32[]{:S(2)}, u32[]{:S(2)}) collective-permute-start(f32[17,16,64]{2,1,0:T(8,128)S(1)} %get-tuple-element.8), channel_id=1, source_target_pairs={{0,2},{1,3},{2,4},{3,5},{4,6},{5,7},{6,8},{7,9},{8,10},{9,11},{10,... | collective-permute-start | bytes 208904 | tf_op jit(solution)/shard_map/ppermute | solution.py:24
  56.0 1.9 %collective-permute-start = (f32[17,16,64]{2,1,0:T(8,128)S(1)}, f32[17,16,64]{2,1,0:T(8,128)S(1)}, u32[]{:S(2)}, u32[]{:S(2)}) collective-permute-start(f32[17,16,64]{2,1,0:T(8,128)S(1)} %get-tuple-element.7), channel_id=1, source_target_pairs={{0,1},{1,2},{2,3},{3,4},{4,5},{5,6},{6,7},{7,8},{8,9},{9,10},{10,1... | collective-permute-start | bytes 208904 | tf_op jit(solution)/shard_map/ppermute | solution.py:24
  57.9 4.1 %collective-permute-done.1 = f32[17,16,64]{2,1,0:T(8,128)S(1)} collective-permute-done((f32[17,16,64]{2,1,0:T(8,128)S(1)}, f32[17,16,64]{2,1,0:T(8,128)S(1)}, u32[]{:S(2)}, u32[]{:S(2)}) %collective-permute-start.1) | collective-permute-done | bytes 69664 | tf_op jit(solution)/shard_map/ppermute | solution.py:24
  62.0 1.4 %collective-permute-done = f32[17,16,64]{2,1,0:T(8,128)S(1)} collective-permute-done((f32[17,16,64]{2,1,0:T(8,128)S(1)}, f32[17,16,64]{2,1,0:T(8,128)S(1)}, u32[]{:S(2)}, u32[]{:S(2)}) %collective-permute-start) | collective-permute-done | bytes 69664 | tf_op jit(solution)/shard_map/ppermute | solution.py:24
  63.4 0.7 %slice_divide_fusion = f32[16,16,64]{2,1,0:T(8,128)} fusion(f32[17,16,64]{2,1,0:T(8,128)S(1)} %fusion.4, f32[16,64]{1,0:T(8,128)S(1)} %fusion.11), kind=kLoop, calls=%fused_computation.8 | loop fusion | flops 16384 | bytes 135168 | tf_op jit(solution)/shard_map/div | solution.py:430
  (4 shorter events, 0.1 us)
Async XLA Ops:
  49.5 2.6 %copy-start = (s32[2,2]{1,0:T(2,128)S(1)}, s32[2,2]{1,0:T(2,128)}, u32[]{:S(2)}) copy-start(s32[2,2]{1,0:T(2,128)} %param.14) | copy-start | bytes 52
  53.4 8.6 %collective-permute-start.1 = (f32[17,16,64]{2,1,0:T(8,128)S(1)}, f32[17,16,64]{2,1,0:T(8,128)S(1)}, u32[]{:S(2)}, u32[]{:S(2)}) collective-permute-start(f32[17,16,64]{2,1,0:T(8,128)S(1)} %get-tuple-element.8), channel_id=1, source_target_pairs={{0,2},{1,3},{2,4},{3,5},{4,6},{5,7},{6,8},{7,9},{8,10},{9,11},{10,... | collective-permute-start | bytes 208904 | tf_op jit(solution)/shard_map/ppermute | solution.py:24
  56.0 7.4 %collective-permute-start = (f32[17,16,64]{2,1,0:T(8,128)S(1)}, f32[17,16,64]{2,1,0:T(8,128)S(1)}, u32[]{:S(2)}, u32[]{:S(2)}) collective-permute-start(f32[17,16,64]{2,1,0:T(8,128)S(1)} %get-tuple-element.7), channel_id=1, source_target_pairs={{0,1},{1,2},{2,3},{3,4},{4,5},{5,6},{6,7},{7,8},{8,9},{9,10},{10,1... | collective-permute-start | bytes 208904 | tf_op jit(solution)/shard_map/ppermute | solution.py:24
where the time goes:
time: 64.3 us; the launch traced here: 64.1 us
  Pallas kernels  48.8 us (76%)
  waiting for transfers between devices  5.48 us (9%)
  starting transfers between devices  4.5 us (7%)
  local copies, waits for them, and re-layouts  2.57 us (4%)
  other arithmetic  1.76 us (3%)
  matrix products  0.88 us (1%)
    pallas_call x1, Pallas kernels, shards(): pl.pallas_call(functools.partial(block_kernel, n), out_shape=jax.ShapeDty...  48.8 us
    ppermute x2, waiting for transfers between devices, shifted(): return lax.ppermute(block, axis, route)  5.48 us
    ppermute x2, starting transfers between devices, shifted(): return lax.ppermute(block, axis, route)  4.5 us
    reshape x2, local copies, waits for them, and re-layouts, shards(): grid = patch_vel.reshape(C, PATCH, PATCH, windows, GRID, GRID)  2.07 us
  transfers between devices with their start and end apart: 2, of which 2 were waited for; matrix products, arithmetic and copies ran while one was open for 0% of the time, Pallas kernels for 0%

commit v1 on v0

v1 whole, which is shorter than its diff:
```python
import functools
import math

import jax
import jax.numpy as jnp
from jax import lax
from jax.experimental import pallas as pl
from jax.experimental.pallas import tpu as pltpu
from jax.sharding import PartitionSpec as P

HD = 128
C = 16
HEADS = 12
PATCH = 2
WIN = 32
LW = 64
BAND = 16
GRID = 16


def shifted(block, axis, distance):
    devices = range(lax.axis_size(axis))
    route = [(i - distance, i) for i in devices if i - distance in devices]
    return lax.ppermute(block, axis, route)


def place_window(canvas, totals, contrib, weights, row_at, col_at):
    zero_index = jnp.zeros((), jnp.int32)
    region = lax.dynamic_slice(canvas, (zero_index, row_at, col_at), (C, WIN, WIN))
    canvas = lax.dynamic_update_slice(canvas, region + contrib, (zero_index, row_at, col_at))
    weight_region = lax.dynamic_slice(totals, (row_at, col_at), (WIN, WIN))
    totals = lax.dynamic_update_slice(totals, weight_region + weights, (row_at, col_at))
    return (canvas, totals)


def fold_columns(field):
    span_cols = field.shape[-1] - WIN
    leading = field[..., :span_cols]
    wrapped = field[..., span_cols:]
    padding = [(0, 0)] * (field.ndim - 1) + [(0, span_cols - WIN)]
    return leading + jnp.pad(wrapped, padding)


def plain_shards(img_qkv, txt_kv, hidden, w_proj, w_out, modulation, anchors, blend_weight):
    window_count, tokens, _ = img_qkv.shape
    features = HEADS * HD
    queries = img_qkv[:, :, :features].reshape(window_count, tokens, HEADS, HD)
    all_keys = jnp.concatenate(
        [txt_kv[:, :, :features], img_qkv[:, :, features : 2 * features]], axis=1
    )
    all_keys = all_keys.reshape(window_count, -1, HEADS, HD)
    all_values = jnp.concatenate([txt_kv[:, :, features:], img_qkv[:, :, 2 * features :]], axis=1)
    all_values = all_values.reshape(window_count, -1, HEADS, HD)
    scores = jnp.einsum(
        "wqhd,wkhd->whqk", queries, all_keys, preferred_element_type=jnp.float32
    ) / math.sqrt(HD)
    scores = scores - jnp.max(scores, axis=-1, keepdims=True)
    exp_scores = jnp.exp(scores)
    soft_weights = (exp_scores / jnp.sum(exp_scores, axis=-1, keepdims=True)).astype(jnp.bfloat16)
    attended = jnp.einsum(
        "whqk,wkhd->wqhd", soft_weights, all_values, preferred_element_type=jnp.float32
    )
    attended = attended.reshape(window_count * tokens, features).astype(jnp.bfloat16)
    whole_proj = lax.all_gather(w_proj, "win", axis=0, tiled=True)
    projected = jnp.dot(attended, whole_proj, preferred_element_type=jnp.float32)
    residual = (
        hidden.reshape(window_count * tokens, -1).astype(jnp.float32) + modulation[0] * projected
    )
    row_mean = jnp.mean(residual, axis=-1, keepdims=True)
    centred = residual - row_mean
    row_var = jnp.mean(centred * centred, axis=-1, keepdims=True)
    normed = centred * lax.rsqrt(row_var + 1e-06)
    modulated = (normed * (1.0 + modulation[1]) + modulation[2]).astype(jnp.bfloat16)
    patch_vel = jnp.dot(modulated, w_out, preferred_element_type=jnp.float32)
    patch_grid = patch_vel.reshape(window_count, GRID, GRID, C, PATCH, PATCH)
    window_vel = patch_grid.transpose(0, 3, 1, 4, 2, 5).reshape(window_count, C, WIN, WIN)
    weights = blend_weight.astype(jnp.float32)
    contrib = window_vel * weights[:, None]
    band_start = lax.axis_index("win") * BAND
    canvas = jnp.zeros((C, BAND + WIN, LW + WIN), jnp.float32)
    totals = jnp.zeros((BAND + WIN, LW + WIN), jnp.float32)

    def add_one(window, running):
        row_at = anchors[window, 0] - band_start
        col_at = anchors[window, 1]
        return place_window(
            running[0], running[1], contrib[window], weights[window], row_at, col_at
        )

    canvas, totals = lax.fori_loop(0, window_count, add_one, (canvas, totals))
    canvas = fold_columns(canvas)
    totals = fold_columns(totals)
    own_canvas = canvas[:, :BAND]
    own_totals = totals[:BAND]
    near_canvas = canvas[:, BAND : 2 * BAND]
    near_totals = totals[BAND : 2 * BAND]
    far_canvas = canvas[:, 2 * BAND :]
    far_totals = totals[2 * BAND :]
    prev_canvas, prev_totals = shifted((near_canvas, near_totals), "win", 1)
    second_canvas, second_totals = shifted((far_canvas, far_totals), "win", 2)
    sum_canvas = own_canvas + prev_canvas + second_canvas
    sum_totals = own_totals + prev_totals + second_totals
    return sum_canvas / jnp.maximum(sum_totals, 1.0)[None]


LOG2E = 1.4426950408889634
MESH_ID = pl.DeviceIdType.MESH


def block_kernel(
    n,
    qkv_hbm,
    txt_hbm,
    hid_hbm,
    wp_hbm,
    wout_hbm,
    mod_hbm,
    anchors_hbm,
    blend_hbm,
    out_ref,
    qkv,
    txt,
    hid,
    weights,
    att,
    left_first,
    left_mid,
    left_last,
    acc,
    wout,
    wperm,
    mod,
    anchors,
    blend,
    cells,
    hot,
    totals,
    total_near,
    total_far,
    sum_one,
    sum_two,
    centre,
    vel,
    feature,
    near_out,
    far_out,
    near_in,
    far_in,
    load_sems,
    cw_send,
    cw_recv,
    ccw_send,
    ccw_recv,
    y_send,
    y_recv,
    part_send,
    part_recv,
    halo_send,
    halo_recv,
):
    windows, tokens, _ = qkv.shape
    rows = wp_hbm.shape[0]
    width = weights.shape[1]
    features = HEADS * HD
    deep = 2 * rows
    unit = width // 6
    half = unit // 2
    chips = n // 2
    reach = chips // 2
    group = lax.axis_index("group")
    me = lax.axis_index("win")
    core = me % 2
    chip = me // 2
    depth, side = chip // 2, chip % 2
    place = depth + side * (chips - 1 - 2 * depth)

    def chip_at(position):
        spot = (position + chips) % chips
        turn = spot // reach
        return 2 * (spot + turn * (chips - 1 - 2 * spot)) + turn

    onward = (group, chip_at(place + 1) * 2 + core)
    backward = (group, chip_at(place - 1) * 2 + core)
    across = (1 - group, me)
    partner = (group, me + 1 - 2 * core)

    def source(way, d):
        return chip_at(place + d) if way else chip_at(place - d)

    def column(way, which, u):
        flip = which * (5 - 2 * u) * unit
        return (5 - u) * unit - flip if way else u * unit + flip

    def region(which_chip, which_core, col, cols):
        row = pl.multiple_of((which_chip * 2 + which_core) * rows, 16)
        return weights.at[pl.ds(row, rows), pl.ds(pl.multiple_of(col, 128), cols)]

    def remote(src, dst, send, recv, device):
        return pltpu.make_async_remote_copy(
            src_ref=src, dst_ref=dst, send_sem=send, recv_sem=recv,
            device_id=device, device_id_type=MESH_ID,
        )

    def ring(way, d, piece, hop):
        if d == reach and piece >= 2:
            col, cols = column(way, group, 2) + (piece - 2) * half, half
        else:
            col, cols = column(way, group, piece), unit
        ref = region(source(way, d - 1 + hop), core, col, cols)
        send, recv = (ccw_send, ccw_recv) if way else (cw_send, cw_recv)
        return remote(
            ref, ref, send.at[d - 1, piece], recv.at[d - 1, piece], backward if way else onward
        )

    def yy(d, u, way, which):
        ref = region(source(way, d), core, column(way, which, u), unit)
        j = ((d - 1) * 2 + u) * 2 + way
        return remote(ref, ref, y_send.at[j], y_recv.at[j], across)

    names = [("own",)]
    for d in range(1, reach):
        for way in range(2):
            names += [("ring", d, way, 0), ("ring", d, way, 1)]
            names += [("far", d, way, 0), ("far", d, way, 1)] if d == reach - 1 else [("both", d, way)]
    for way in range(2):
        names += [("last", way, piece) for piece in range(4)]
    spot_of = {name: i for i, name in enumerate(names)}

    def part(name, which_core):
        kind = name[0]
        if kind == "own":
            ref = region(chip, which_core, 0, width)
        elif kind == "ring":
            _, d, way, upper = name
            low = jnp.minimum(column(way, group, 0), column(way, group, 1))
            col = 2 * unit if upper else low
            ref = region(source(way, d), which_core, col, 2 * unit)
        elif kind == "both":
            _, d, way = name
            low = jnp.minimum(column(way, 1 - group, 0), column(way, 1 - group, 1))
            ref = region(source(way, d), which_core, low, 2 * unit)
        elif kind == "far":
            _, d, way, u = name
            ref = region(source(way, d), which_core, column(way, 1 - group, u), unit)
        else:
            _, way, piece = name
            if piece >= 2:
                ref = region(
                    source(way, reach), which_core, column(way, group, 2) + (piece - 2) * half, half
                )
            else:
                ref = region(source(way, reach), which_core, column(way, group, piece), unit)
        i = spot_of[name]
        return remote(ref, ref, part_send.at[i], part_recv.at[i], partner)

    landed = set()

    def need(*wanted):
        for name in wanted:
            if name not in landed:
                landed.add(name)
                part(name, 1 - core).wait_recv()

    own_load = pltpu.make_async_copy(wp_hbm, region(chip, core, 0, width), load_sems.at[0])
    own_load.start()
    loads = []
    for w in range(windows):
        loads.append(
            (
                pltpu.make_async_copy(qkv_hbm.at[w], qkv.at[w], load_sems.at[1 + 2 * w]),
                pltpu.make_async_copy(txt_hbm.at[w], txt.at[w], load_sems.at[2 + 2 * w]),
            )
        )
    base = 1 + 2 * windows
    side_loads = [
        pltpu.make_async_copy(wout_hbm, wout, load_sems.at[base]),
        pltpu.make_async_copy(mod_hbm, mod, load_sems.at[base + 1]),
        pltpu.make_async_copy(anchors_hbm, anchors, load_sems.at[base + 2]),
        pltpu.make_async_copy(blend_hbm, blend, load_sems.at[base + 3]),
    ]
    hid_load = pltpu.make_async_copy(hid_hbm, hid, load_sems.at[base + 4])

    barrier = pltpu.get_barrier_semaphore()
    after = [(group, (me + 1) % n), (group, (me + 2) % n)]
    before = [(group, (me + n - 1) % n), (group, (me + n - 2) % n)]
    greeted = [onward, backward, across, partner] + after + before
    for device in greeted:
        pl.semaphore_signal(barrier, inc=1, device_id=device, device_id_type=MESH_ID)
    for copy in loads[0]:
        copy.start()
    pl.semaphore_wait(barrier, len(greeted))

    own_load.wait()
    for piece in range(4):
        ring(0, 1, piece, 0).start()
        ring(1, 1, piece, 0).start()
    part(("own",), core).start()
    for pair in loads[1:]:
        for copy in pair:
            copy.start()
    for copy in side_loads:
        copy.start()
    hid_load.start()

    scale = LOG2E / math.sqrt(HD)

    def attend(w, h):
        col = pl.multiple_of(h * HD, HD)
        cols = pl.ds(col, HD)
        kcols = pl.ds(pl.multiple_of(col + features, HD), HD)
        vcols = pl.ds(pl.multiple_of(col + 2 * features, HD), HD)
        q = qkv[w, :, cols]
        dims = (((1,), (1,)), ((), ()))
        st = lax.dot_general(txt[w, :, cols], q, dims, preferred_element_type=jnp.float32)
        si = lax.dot_general(qkv[w, :, kcols], q, dims, preferred_element_type=jnp.float32)
        top = jnp.maximum(jnp.max(st, axis=0, keepdims=True), jnp.max(si, axis=0, keepdims=True))
        pt = jnp.exp2((st - top) * scale)
        pi = jnp.exp2((si - top) * scale)
        total = jnp.sum(pt, axis=0, keepdims=True) + jnp.sum(pi, axis=0, keepdims=True)
        back = (((0,), (0,)), ((), ()))
        out = lax.dot_general(
            txt[w, :, kcols], pt.astype(jnp.bfloat16), back, preferred_element_type=jnp.float32
        ) + lax.dot_general(
            qkv[w, :, vcols], pi.astype(jnp.bfloat16), back, preferred_element_type=jnp.float32
        )
        att[pl.ds(col, HD), pl.ds(pl.multiple_of(w * tokens, 128), tokens)] = (
            out * (1.0 / total)
        ).astype(jnp.bfloat16)

    def spot(which_chip):
        return pl.ds(pl.multiple_of(which_chip * deep, 16), deep)

    def turn_left():
        def turned(chips_held):
            return jnp.concatenate([att[spot(c), :] for c in chips_held], axis=0).T

        left_first[...] = turned([chip, source(0, 1), source(1, 1)])
        for d in range(2, reach):
            left_mid[d - 2] = turned([source(0, d), source(1, d)])
        left_last[...] = turned([source(0, reach)])

    def right(chips_held, at):
        return jnp.concatenate([weights[spot(c), at] for c in chips_held], axis=0)

    def project_first(t):
        at = pl.ds(t * unit, unit)
        held = [chip, source(0, 1), source(1, 1)]
        acc[:, at] = jnp.dot(left_first[...], right(held, at), preferred_element_type=jnp.float32)

    def project_mid(d, t):
        at = pl.ds(t * unit, unit)
        held = [source(0, d), source(1, d)]
        acc[:, at] += jnp.dot(
            left_mid[d - 2], right(held, at), preferred_element_type=jnp.float32
        )

    def finalize(t, piece, first=False):
        at = pl.ds(t * unit + piece * half, half)
        term = acc[:, at] + jnp.dot(
            left_last[...], right([source(0, reach)], at), preferred_element_type=jnp.float32
        )
        residual = hid[:, at].astype(jnp.float32) + mod[0:1, at] * term
        if first:
            mean = jnp.sum(residual, axis=-1, keepdims=True) * (1.0 / half)
            centre[...] = jnp.broadcast_to(mean, centre.shape)
        lanes = centre.shape[1]
        pieces = [residual[:, i : i + lanes] - centre[...] for i in range(0, half, lanes)]
        one = functools.reduce(lambda a, b: a + b, pieces)
        two = functools.reduce(lambda a, b: a + b, [x * x for x in pieces])
        sum_one[...] = one if first else sum_one[...] + one
        sum_two[...] = two if first else sum_two[...] + two
        scaled = (jnp.concatenate(pieces, axis=1) * (1.0 + mod[1:2, at])).astype(jnp.bfloat16)
        term = lax.dot_general(
            wperm[:, at], scaled, (((1,), (1,)), ((), ())), preferred_element_type=jnp.float32
        )
        vel[...] = term if first else vel[...] + term

    grid_log = GRID.bit_length() - 1
    spread = hot.shape[2]
    band = spread // 3
    outs = wout.shape[0]

    def parity(w):
        row_at = anchors[w : w + 1, 0:1] - me * BAND
        return row_at & 1, row_at >> 1, anchors[w : w + 1, 1:2]

    def prepare_weights():
        for copy in side_loads:
            copy.wait()
        order = lax.broadcasted_iota(jnp.int32, (outs, outs), 0)
        taken = lax.broadcasted_iota(jnp.int32, (outs, outs), 1)
        wanted = (order % C) * (PATCH * PATCH) + order // C
        permute = (taken == wanted).astype(jnp.bfloat16)
        wperm[...] = jnp.dot(permute, wout[...], preferred_element_type=jnp.float32).astype(
            jnp.bfloat16
        )
        plain = wperm[...].astype(jnp.float32)
        gain = jnp.sum(plain * (1.0 + mod[1:2, :]), axis=-1, keepdims=True)
        shift = jnp.sum(plain * mod[2:3, :], axis=-1, keepdims=True)
        feature[0] = jnp.broadcast_to(gain, feature.shape[1:])
        feature[1] = jnp.broadcast_to(shift, feature.shape[1:])
        token = lax.broadcasted_iota(jnp.int32, (WIN, tokens), 1)
        line = lax.broadcasted_iota(jnp.int32, (WIN, tokens), 0)
        for w in range(windows):
            held = blend[w].astype(jnp.float32).astype(jnp.bfloat16)
            for b in range(PATCH):
                pick = (line == PATCH * (token & (GRID - 1)) + b).astype(jnp.bfloat16)
                wide = jnp.dot(held, pick, preferred_element_type=jnp.float32)
                for a in range(PATCH):
                    mine = jnp.where(line == PATCH * (token >> grid_log) + a, wide, 0.0)
                    row = jnp.sum(mine, axis=0, keepdims=True)
                    cells[a * PATCH + b, :, w * tokens : (w + 1) * tokens] = jnp.broadcast_to(
                        row, (8, tokens)
                    )

    def prepare_hot(alpha):
        token = lax.broadcasted_iota(jnp.int32, (tokens, 128), 0)
        lane = lax.broadcasted_iota(jnp.int32, (tokens, 128), 1)
        for w in range(windows):
            odd, row_at, col_at = parity(w)
            tall = (token >> grid_log) + row_at + odd * (1 - alpha)
            for b in range(PATCH):
                wide = (PATCH * (token & (GRID - 1)) + b + col_at) & (LW - 1)
                target = tall * LW + wide - lane
                for j in range(spread // 128):
                    hot[alpha * PATCH + b, w * tokens : (w + 1) * tokens, j * 128 : (j + 1) * 128] = (
                        jnp.where(target == j * 128, 1.0, 0.0).astype(jnp.bfloat16)
                    )

    def by_parity(w, straight, swapped):
        odd = parity(w)[0]
        return jnp.where(jnp.broadcast_to(odd, straight.shape) == 0, straight, swapped)

    def prepare_totals():
        found = []
        for alpha in range(PATCH):
            total = jnp.zeros((8, spread), jnp.float32)
            for b in range(PATCH):
                held = []
                for w in range(windows):
                    at = slice(w * tokens, (w + 1) * tokens)
                    straight = cells[alpha * PATCH + b, :, at]
                    swapped = cells[(1 - alpha) * PATCH + b, :, at]
                    held.append(by_parity(w, straight, swapped))
                left = jnp.concatenate(held, axis=1).astype(jnp.bfloat16)
                total += jnp.dot(
                    left, hot[alpha * PATCH + b], preferred_element_type=jnp.float32
                )
            found.append(total)
        upper = lax.broadcasted_iota(jnp.int32, (8, spread), 0) < 4
        total = jnp.where(upper, found[0], found[1])
        for i in range(3):
            totals[i] = total[:, i * band : (i + 1) * band]

    halos = (
        (1, remote(totals.at[1], total_near, halo_send.at[0], halo_recv.at[0], after[0])),
        (2, remote(totals.at[2], total_far, halo_send.at[1], halo_recv.at[1], after[1])),
        (1, remote(near_out, near_in, halo_send.at[2], halo_recv.at[2], after[0])),
        (2, remote(far_out, far_in, halo_send.at[3], halo_recv.at[3], after[1])),
    )

    def send_halo(i):
        ahead, copy = halos[i]

        @pl.when(me + ahead < n)
        def _():
            copy.start()

    def take_halo(i):
        ahead, copy = halos[i]

        @pl.when(me >= ahead)
        def _():
            copy.wait_recv()

    def close_halo(i):
        ahead, copy = halos[i]

        @pl.when(me + ahead < n)
        def _():
            copy.wait_send()

    def clear_halos():
        @pl.when(me < 1)
        def _():
            total_near[...] = jnp.zeros_like(total_near)
            near_in[...] = jnp.zeros_like(near_in)

        @pl.when(me < 2)
        def _():
            total_far[...] = jnp.zeros_like(total_far)
            far_in[...] = jnp.zeros_like(far_in)

    def send_totals():
        send_halo(0)
        send_halo(1)

    def close_totals():
        take_halo(0)
        take_halo(1)
        summed = totals[0] + total_near[...] + total_far[...]
        totals[0] = 1.0 / jnp.maximum(summed, 1.0)

    slots = [(d, u) for d in range(1, reach) for u in range(4)]
    slots += [(reach, piece) for piece in range(4)]
    across_order = [(d, u, way) for d in range(1, reach) for u in range(2) for way in range(2)]

    def serve(d, piece):
        for way in range(2):
            ring(way, d, piece, 1).wait_recv()
            if d + 1 < reach or (d + 1 == reach and piece < 2):
                ring(way, d + 1, piece, 0).start()
            elif d + 1 == reach and piece == 2:
                ring(way, reach, 2, 0).start()
                ring(way, reach, 3, 0).start()
            if d < reach and piece < 2:
                yy(d, piece, way, group).start()
        for way in range(2):
            if d < reach and piece % 2 == 1:
                part(("ring", d, way, piece // 2), core).start()
            elif d == reach:
                part(("last", way, piece), core).start()

    def serve_across(j):
        d, u, way = across_order[j]
        yy(d, u, way, 1 - group).wait_recv()
        if d == reach - 1:
            part(("far", d, way, u), core).start()
        elif u == 1:
            part(("both", d, way), core).start()

    units = [(w, h) for w in range(windows) for h in range(HEADS)]
    ready = set()

    def attend_some(count):
        for _ in range(min(count, len(units))):
            w, h = units.pop(0)
            if w not in ready:
                for copy in loads[w]:
                    copy.wait()
                ready.add(w)
            attend(w, h)

    def first_ones(which):
        need(("own",))
        for way in range(2):
            need(("ring", 1, way, 0), ("ring", 1, way, 1), ("both", 1, way))
        for t in which:
            project_first(t)

    def mid_ones(d, which):
        for way in range(2):
            need(("ring", d, way, 0), ("ring", d, way, 1))
            if d < reach - 1:
                need(("both", d, way))
        for t in which:
            project_mid(d, t)

    last = reach - 1
    total_slots = len(slots)
    work = {i: [] for i in range(total_slots + 1)}
    per = -(-len(units) // 5)
    for i in range(5):
        work[i].append(functools.partial(attend_some, per))
    work[5] += [functools.partial(attend_some, len(units)), turn_left, prepare_weights, clear_halos]
    work[6] += [functools.partial(prepare_hot, 0), functools.partial(prepare_hot, 1)]
    work[7] += [prepare_totals, send_totals, hid_load.wait]
    work[8] += [functools.partial(first_ones, range(3))]
    work[9] += [functools.partial(first_ones, range(3, 6))]
    work[10] += [close_totals]
    for d in range(2, last):
        at = 4 * d + 4
        work[at] += [functools.partial(mid_ones, d, range(6))]

    def third_middle():
        mid_ones(last, (2, 3))

    def end_outer():
        for way in range(2):
            need(("far", last, way, 0), ("last", way, 0))
        for i, t in enumerate((0, 5)):
            project_mid(last, t)
            for piece in range(2):
                finalize(t, piece, first=i == 0 and piece == 0)

    def end_inner(t):
        for way in range(2):
            need(("far", last, way, 1), ("last", way, 1))
        project_mid(last, t)
        for piece in range(2):
            finalize(t, piece)

    def end_middle(piece):
        for way in range(2):
            need(("last", way, 2 + piece))
        for t in (2, 3):
            finalize(t, piece)

    across_done = 0
    for i, (d, piece) in enumerate(slots):
        for step in work[i]:
            step()
        if i == total_slots - 3:
            third_middle()
            end_outer()
        if i == total_slots - 1:
            end_inner(1)
        serve(d, piece)
        until = max(0, i - 2) if i < total_slots - 3 else len(across_order)
        if i == total_slots - 4:
            until = i - 2 + 1
        until = min(until, len(across_order))
        while across_done < until:
            serve_across(across_done)
            across_done += 1
    end_inner(4)
    end_middle(0)
    end_middle(1)

    flat_one = jnp.sum(sum_one[...].T, axis=0, keepdims=True) * (1.0 / width)
    flat_two = jnp.sum(sum_two[...].T, axis=0, keepdims=True) * (1.0 / width)
    rate = lax.rsqrt(flat_two - flat_one * flat_one + 1e-06)
    gain = jnp.concatenate([feature[0]] * (windows * tokens // 128), axis=1)
    shift = jnp.concatenate([feature[1]] * (windows * tokens // 128), axis=1)
    value = rate * (vel[...] - flat_one * gain) + shift
    weighted = []
    for q in range(PATCH * PATCH):
        cell = jnp.concatenate([cells[q]] * (C // 8), axis=0)
        weighted.append(value[q * C : (q + 1) * C] * cell)
    chosen = []
    for alpha in range(PATCH):
        for b in range(PATCH):
            held = []
            for w in range(windows):
                at = slice(w * tokens, (w + 1) * tokens)
                straight = weighted[alpha * PATCH + b][:, at]
                swapped = weighted[(1 - alpha) * PATCH + b][:, at]
                held.append(by_parity(w, straight, swapped))
            both = jnp.concatenate(held, axis=1)
            high = both.astype(jnp.bfloat16)
            low = (both - high.astype(jnp.float32)).astype(jnp.bfloat16)
            chosen.append(jnp.concatenate([high, low], axis=0))

    def placed(alpha, which):
        total = jnp.zeros((2 * C, band), jnp.float32)
        for b in range(PATCH):
            total += jnp.dot(
                chosen[alpha * PATCH + b],
                hot[alpha * PATCH + b, :, which * band : (which + 1) * band],
                preferred_element_type=jnp.float32,
            )
        return total[:C] + total[C:]

    for which, ref, halo in ((2, far_out, 3), (1, near_out, 2)):
        for alpha in range(PATCH):
            ref[alpha * C : (alpha + 1) * C, :] = placed(alpha, which)
        send_halo(halo)
    own = [placed(alpha, 0) for alpha in range(PATCH)]
    inverse = totals[0]
    take_halo(2)
    take_halo(3)
    for alpha in range(PATCH):
        at = slice(alpha * C, (alpha + 1) * C)
        summed = (own[alpha] + near_in[at, :] + far_in[at, :]) * inverse[4 * alpha : 4 * alpha + 1, :]
        for i in range(band // LW):
            out_ref[pl.ds(PATCH * i + alpha, C, stride=BAND), :] = summed[:, i * LW : (i + 1) * LW]

    for d, piece in slots:
        for way in range(2):
            ring(way, d, piece, 0).wait_send()
    for d, u, way in across_order:
        yy(d, u, way, group).wait_send()
    for name in names:
        part(name, core).wait_send()
    for i in range(len(halos)):
        close_halo(i)


def shards(n, img_qkv, txt_kv, hidden, w_proj, w_out, modulation, anchors, blend_weight):
    windows, tokens, qkv_width = img_qkv.shape
    rows, width = w_proj.shape
    total = windows * tokens
    reach = n // 4
    deep = 2 * rows
    outs = w_out.shape[1]
    spread = (BAND + WIN) // PATCH * LW
    band = spread // 3
    any_space = pl.BlockSpec(memory_space=pl.ANY)
    vmem = pl.BlockSpec(memory_space=pltpu.VMEM)
    dma = pltpu.SemaphoreType.DMA
    f32, bf16 = jnp.float32, jnp.bfloat16
    parts = 1 + 6 * (reach - 2) + 8 + 8
    velocity = pl.pallas_call(
        functools.partial(block_kernel, n),
        out_shape=jax.ShapeDtypeStruct((C * BAND, LW), f32),
        in_specs=[any_space] * 8,
        out_specs=vmem,
        scratch_shapes=[
            pltpu.VMEM(img_qkv.shape, bf16),
            pltpu.VMEM(txt_kv.shape, bf16),
            pltpu.VMEM((total, width), bf16),
            pltpu.VMEM((n * rows, width), bf16),
            pltpu.VMEM((n * rows, total), bf16),
            pltpu.VMEM((total, 3 * deep), bf16),
            pltpu.VMEM((reach - 2, total, 2 * deep), bf16),
            pltpu.VMEM((total, deep), bf16),
            pltpu.VMEM((total, width), f32),
            pltpu.VMEM((outs, width), bf16),
            pltpu.VMEM((outs, width), bf16),
            pltpu.VMEM(modulation.shape, f32),
            pltpu.VMEM(anchors.shape, jnp.int32),
            pltpu.VMEM(blend_weight.shape, jnp.int32),
            pltpu.VMEM((PATCH * PATCH, 8, total), f32),
            pltpu.VMEM((PATCH * PATCH, total, spread), bf16),
            pltpu.VMEM((3, 8, band), f32),
            pltpu.VMEM((8, band), f32),
            pltpu.VMEM((8, band), f32),
            pltpu.VMEM((total, 128), f32),
            pltpu.VMEM((total, 128), f32),
            pltpu.VMEM((total, 128), f32),
            pltpu.VMEM((outs, total), f32),
            pltpu.VMEM((2, outs, 128), f32),
            pltpu.VMEM((PATCH * C, band), f32),
            pltpu.VMEM((PATCH * C, band), f32),
            pltpu.VMEM((PATCH * C, band), f32),
            pltpu.VMEM((PATCH * C, band), f32),
            dma((6 + 2 * windows,)),
            dma((reach, 4)),
            dma((reach, 4)),
            dma((reach, 4)),
            dma((reach, 4)),
            dma((4 * (reach - 1),)),
            dma((4 * (reach - 1),)),
            dma((parts,)),
            dma((parts,)),
            dma((4,)),
            dma((4,)),
        ],
        compiler_params=pltpu.CompilerParams(
            collective_id=0, has_side_effects=True, vmem_limit_bytes=60 * 1024 * 1024
        ),
    )(
        img_qkv,
        txt_kv,
        hidden.reshape(total, width),
        w_proj,
        w_out.T,
        modulation,
        anchors,
        blend_weight,
    )
    return velocity.reshape(C, BAND, LW)


def solution(mesh):
    in_specs = (
        P(("group", "win"), None, None),
        P(("group", "win"), None, None),
        P(("group", "win"), None, None),
        P("win", None),
        P(),
        P("group", None),
        P(("group", "win"), None),
        P(("group", "win"), None, None),
    )
    out_specs = P(None, ("group", "win"), None)
    n = mesh.shape["win"]

    def body(*args):
        rows, width = args[3].shape
        ringed = (
            mesh.shape["group"] == 2
            and n % 4 == 0
            and n >= 16
            and rows % 16 == 0
            and width % 1536 == 0
        )
        if ringed:
            return shards(n, *args)
        return plain_shards(*args)

    return jax.shard_map(body, mesh=mesh, in_specs=in_specs, out_specs=out_specs, check_vma=False)
```

time: 64.3 us -> 50.8 us (0.79)
  waiting for transfers between devices: 5.48 us -> 0 us
  starting transfers between devices: 4.5 us -> 0 us
  other arithmetic: 1.76 us -> 0 us
  local copies, waits for them, and re-layouts: 2.57 us -> 1.57 us
  matrix products: 0.88 us -> 0 us
    ppermute x2 -> x0, waiting for transfers between devices: 5.48 us -> none  [shifted(): return lax.ppermute(block, axis, route)]
    ppermute x2 -> x0, starting transfers between devices: 4.5 us -> none  [shifted(): return lax.ppermute(block, axis, route)]
    reshape x3 -> x0, local copies, waits for them, and re-layouts: 2.54 us -> none  [the longest x2 2.07 us: shards(): grid = patch_vel.reshape(C, PATCH, PATCH, windows, GRID, GRID)]
    unnamed x2 -> x1, local copies, waits for them, and re-layouts: 0.01 us -> 1.57 us
    dot_general x2 -> x0, matrix products: 0.88 us -> none  [the longest x1 0.44 us: shards(): jnp.einsum('wcas,war->crs', wide, row_hot, precision=lax.Precision.HIGHEST)]
    convert_element_type x1 -> x0, other arithmetic: 0.76 us -> none  [shards(): weights = blend_weight.astype(jnp.float32)]
    div x2 -> x0, other arithmetic: 0.68 us -> none  [shards(): return summed[:C] / jnp.maximum(summed[C], 1.0)[None]]
  transfers between devices with their start and end apart: 2 -> 0, of which waited for: 2 -> 0; matrix products, arithmetic and copies ran while one was open for 0% -> 0% of each run, Pallas kernels for 0% -> 0%
where the time goes in v1:
time: 50.8 us; the launch traced here: 50.7 us
  Pallas kernels  49.1 us (97%)
  local copies, waits for them, and re-layouts  1.57 us (3%)
    pallas_call x1, Pallas kernels, shards(): pl.pallas_call(functools.partial(block_kernel, n), out_shape=jax.ShapeDty...  49.1 us
    unnamed x1, local copies, waits for them, and re-layouts  1.57 us

profile of v1, /device:TPU:8, one launch (start us, length us, event | category | flops | bytes accessed | tf_op | source)
XLA Modules:
  0.0 50.7 jit_solution(6244933609696167670)
XLA Ops:
  0.0 49.1 %shard_map.82 = f32[256,64]{1,0:T(8,128)} custom-call(bf16[2,256,4608]{2,1,0:T(8,128)(2,1)} %qkv_hbm.1, bf16[2,128,3072]{2,1,0:T(8,128)(2,1)} %txt_hbm.1, bf16[512,3072]{1,0:T(8,128)(2,1)} %bitcast.3, bf16[96,3072]{1,0:T(8,128)(2,1)} %wp_hbm.1, bf16[64,3072]{1,0:T(8,128)(2,1)} %bitcast.5, f32[3,3072]{1,0:T(4,128)} %mod_hbm.1, s32[2,2]{1,0:T(2,128)} %anchors_hbm.1, ...), custom_call_target="tpu_custom_call" | custom-call | tf_op jit(solution)/shard_map/pallas_call | solution.py:693
  49.1 1.6 %copy.10 = f32[16,16,64]{2,1,0:T(8,128)} copy(f32[16,16,64]{2,1,0:T(8,128)} %bitcast.4) | data formatting | bytes 131072

commit v2 on v1

--- a/solution.py
+++ b/solution.py
@@ -137,7 +137,6 @@
     totals,
     total_near,
     total_far,
-    sum_one,
     sum_two,
     centre,
     vel,
@@ -165,6 +164,7 @@
     deep = 2 * rows
     unit = width // 6
     half = unit // 2
+    outs = wout.shape[0]
     chips = n // 2
     reach = chips // 2
     group = lax.axis_index("group")
@@ -201,20 +201,26 @@
             device_id=device, device_id_type=MESH_ID,
         )
 
+    def cut(way, which, piece):
+        u, side_of = piece
+        col = column(way, which, u)
+        return (col, unit) if side_of is None else (col + side_of * half, half)
+
+    def mark(piece):
+        return 4 if piece[1] == 1 else piece[0]
+
     def ring(way, d, piece, hop):
-        if d == reach and piece >= 2:
-            col, cols = column(way, group, 2) + (piece - 2) * half, half
-        else:
-            col, cols = column(way, group, piece), unit
-        ref = region(source(way, d - 1 + hop), core, col, cols)
+        ref = region(source(way, d - 1 + hop), core, *cut(way, group, piece))
         send, recv = (ccw_send, ccw_recv) if way else (cw_send, cw_recv)
-        return remote(
-            ref, ref, send.at[d - 1, piece], recv.at[d - 1, piece], backward if way else onward
-        )
-
-    def yy(d, u, way, which):
-        ref = region(source(way, d), core, column(way, which, u), unit)
-        j = ((d - 1) * 2 + u) * 2 + way
+        i = mark(piece)
+        return remote(ref, ref, send.at[d - 1, i], recv.at[d - 1, i], backward if way else onward)
+
+    def yy(d, piece, way, which):
+        ref = region(source(way, d), core, *cut(way, which, piece))
+        i = mark(piece)
+        if i == 4:
+            i = 2
+        j = ((d - 1) * 3 + i) * 2 + way
         return remote(ref, ref, y_send.at[j], y_recv.at[j], across)
 
     names = [("own",)]
@@ -223,7 +229,8 @@
             names += [("ring", d, way, 0), ("ring", d, way, 1)]
             names += [("far", d, way, 0), ("far", d, way, 1)] if d == reach - 1 else [("both", d, way)]
     for way in range(2):
-        names += [("last", way, piece) for piece in range(4)]
+        names += [("last", way, 0, None), ("last", way, 1, None)]
+        names += [("last", way, 2, 0), ("last", way, 2, 1)]
     spot_of = {name: i for i, name in enumerate(names)}
 
     def part(name, which_core):
@@ -243,13 +250,8 @@
             _, d, way, u = name
             ref = region(source(way, d), which_core, column(way, 1 - group, u), unit)
         else:
-            _, way, piece = name
-            if piece >= 2:
-                ref = region(
-                    source(way, reach), which_core, column(way, group, 2) + (piece - 2) * half, half
-                )
-            else:
-                ref = region(source(way, reach), which_core, column(way, group, piece), unit)
+            _, way, u, side_of = name
+            ref = region(source(way, reach), which_core, *cut(way, group, (u, side_of)))
         i = spot_of[name]
         return remote(ref, ref, part_send.at[i], part_recv.at[i], partner)
 
@@ -282,18 +284,30 @@
 
     barrier = pltpu.get_barrier_semaphore()
     after = [(group, (me + 1) % n), (group, (me + 2) % n)]
-    before = [(group, (me + n - 1) % n), (group, (me + n - 2) % n)]
-    greeted = [onward, backward, across, partner] + after + before
-    for device in greeted:
+    expected = 4
+    for device in (onward, backward, across, partner):
         pl.semaphore_signal(barrier, inc=1, device_id=device, device_id_type=MESH_ID)
+    for ahead in (-2, -1, 1, 2):
+        there = (me + ahead >= 0) & (me + ahead < n)
+
+        @pl.when(there)
+        def _():
+            pl.semaphore_signal(
+                barrier, inc=1, device_id=(group, (me + ahead + n) % n), device_id_type=MESH_ID
+            )
+
+        expected = expected + there.astype(jnp.int32)
     for copy in loads[0]:
         copy.start()
-    pl.semaphore_wait(barrier, len(greeted))
+    pl.semaphore_wait(barrier, expected)
 
     own_load.wait()
-    for piece in range(4):
-        ring(0, 1, piece, 0).start()
-        ring(1, 1, piece, 0).start()
+    slots = [(1, (0, 0)), (1, (0, 1)), (1, (1, None)), (1, (2, None)), (1, (3, None))]
+    slots += [(d, (u, None)) for d in range(2, reach) for u in range(4)]
+    slots += [(reach, (0, None)), (reach, (1, None)), (reach, (2, 0)), (reach, (2, 1))]
+    for d, piece in slots[:5]:
+        ring(0, d, piece, 0).start()
+        ring(1, d, piece, 0).start()
     part(("own",), core).start()
     for pair in loads[1:]:
         for copy in pair:
@@ -350,35 +364,35 @@
     def project_mid(d, t):
         at = pl.ds(t * unit, unit)
         held = [source(0, d), source(1, d)]
-        acc[:, at] += jnp.dot(
-            left_mid[d - 2], right(held, at), preferred_element_type=jnp.float32
-        )
+        term = jnp.dot(left_mid[d - 2], right(held, at), preferred_element_type=jnp.float32)
+        if d == 2:
+            acc[:, at] = hid[:, at].astype(jnp.float32) + mod[0:1, at] * (acc[:, at] + term)
+        else:
+            acc[:, at] += mod[0:1, at] * term
 
     def finalize(t, piece, first=False):
         at = pl.ds(t * unit + piece * half, half)
-        term = acc[:, at] + jnp.dot(
+        term = jnp.dot(
             left_last[...], right([source(0, reach)], at), preferred_element_type=jnp.float32
         )
-        residual = hid[:, at].astype(jnp.float32) + mod[0:1, at] * term
+        residual = acc[:, at] + mod[0:1, at] * term
         if first:
             mean = jnp.sum(residual, axis=-1, keepdims=True) * (1.0 / half)
             centre[...] = jnp.broadcast_to(mean, centre.shape)
         lanes = centre.shape[1]
         pieces = [residual[:, i : i + lanes] - centre[...] for i in range(0, half, lanes)]
-        one = functools.reduce(lambda a, b: a + b, pieces)
         two = functools.reduce(lambda a, b: a + b, [x * x for x in pieces])
-        sum_one[...] = one if first else sum_one[...] + one
         sum_two[...] = two if first else sum_two[...] + two
-        scaled = (jnp.concatenate(pieces, axis=1) * (1.0 + mod[1:2, at])).astype(jnp.bfloat16)
+        moved = jnp.concatenate(pieces, axis=1).astype(jnp.bfloat16)
         term = lax.dot_general(
-            wperm[:, at], scaled, (((1,), (1,)), ((), ())), preferred_element_type=jnp.float32
+            wperm[:, at], moved, (((1,), (1,)), ((), ())), preferred_element_type=jnp.float32
         )
+        term = jnp.concatenate([term[:outs] + term[outs : 2 * outs], term[2 * outs :]], axis=0)
         vel[...] = term if first else vel[...] + term
 
     grid_log = GRID.bit_length() - 1
     spread = hot.shape[2]
     band = spread // 3
-    outs = wout.shape[0]
 
     def parity(w):
         row_at = anchors[w : w + 1, 0:1] - me * BAND
@@ -391,11 +405,13 @@
         taken = lax.broadcasted_iota(jnp.int32, (outs, outs), 1)
         wanted = (order % C) * (PATCH * PATCH) + order // C
         permute = (taken == wanted).astype(jnp.bfloat16)
-        wperm[...] = jnp.dot(permute, wout[...], preferred_element_type=jnp.float32).astype(
-            jnp.bfloat16
-        )
-        plain = wperm[...].astype(jnp.float32)
-        gain = jnp.sum(plain * (1.0 + mod[1:2, :]), axis=-1, keepdims=True)
+        plain = jnp.dot(permute, wout[...], preferred_element_type=jnp.float32)
+        gained = plain * (1.0 + mod[1:2, :])
+        high = gained.astype(jnp.bfloat16)
+        wperm[:outs, :] = high
+        wperm[outs : 2 * outs, :] = (gained - high.astype(jnp.float32)).astype(jnp.bfloat16)
+        wperm[2 * outs :, :] = jnp.ones((wperm.shape[0] - 2 * outs, width), jnp.bfloat16)
+        gain = jnp.sum(gained, axis=-1, keepdims=True)
         shift = jnp.sum(plain * mod[2:3, :], axis=-1, keepdims=True)
         feature[0] = jnp.broadcast_to(gain, feature.shape[1:])
         feature[1] = jnp.broadcast_to(shift, feature.shape[1:])
@@ -501,29 +517,38 @@
         summed = totals[0] + total_near[...] + total_far[...]
         totals[0] = 1.0 / jnp.maximum(summed, 1.0)
 
-    slots = [(d, u) for d in range(1, reach) for u in range(4)]
-    slots += [(reach, piece) for piece in range(4)]
-    across_order = [(d, u, way) for d in range(1, reach) for u in range(2) for way in range(2)]
+    across_order = [(1, (0, 0), 0), (1, (0, 0), 1), (1, (0, 1), 0), (1, (0, 1), 1)]
+    across_order += [
+        (d, (u, None), way)
+        for d in range(1, reach)
+        for u in range(2)
+        for way in range(2)
+        if (d, u) != (1, 0)
+    ]
 
     def serve(d, piece):
+        u, side_of = piece
         for way in range(2):
             ring(way, d, piece, 1).wait_recv()
-            if d + 1 < reach or (d + 1 == reach and piece < 2):
+            if d == 1 and u == 0:
+                if side_of == 1:
+                    ring(way, 2, (0, None), 0).start()
+            elif d + 1 < reach or (d + 1 == reach and u < 2):
                 ring(way, d + 1, piece, 0).start()
-            elif d + 1 == reach and piece == 2:
-                ring(way, reach, 2, 0).start()
-                ring(way, reach, 3, 0).start()
-            if d < reach and piece < 2:
+            elif d + 1 == reach and u == 2:
+                ring(way, reach, (2, 0), 0).start()
+                ring(way, reach, (2, 1), 0).start()
+            if d < reach and u < 2:
                 yy(d, piece, way, group).start()
         for way in range(2):
-            if d < reach and piece % 2 == 1:
-                part(("ring", d, way, piece // 2), core).start()
+            if d < reach and u % 2 == 1:
+                part(("ring", d, way, u // 2), core).start()
             elif d == reach:
-                part(("last", way, piece), core).start()
+                part(("last", way, u, side_of), core).start()
 
     def serve_across(j):
-        d, u, way = across_order[j]
-        yy(d, u, way, 1 - group).wait_recv()
+        d, (u, side_of), way = across_order[j]
+        yy(d, (u, side_of), way, 1 - group).wait_recv()
         if d == reach - 1:
             part(("far", d, way, u), core).start()
         elif u == 1:
@@ -557,72 +582,84 @@
             project_mid(d, t)
 
     last = reach - 1
-    total_slots = len(slots)
-    work = {i: [] for i in range(total_slots + 1)}
-    per = -(-len(units) // 5)
-    for i in range(5):
-        work[i].append(functools.partial(attend_some, per))
-    work[5] += [functools.partial(attend_some, len(units)), turn_left, prepare_weights, clear_halos]
-    work[6] += [functools.partial(prepare_hot, 0), functools.partial(prepare_hot, 1)]
-    work[7] += [prepare_totals, send_totals, hid_load.wait]
-    work[8] += [functools.partial(first_ones, range(3))]
-    work[9] += [functools.partial(first_ones, range(3, 6))]
-    work[10] += [close_totals]
+
+    def third(which, *kinds):
+        for way in range(2):
+            need(*[(kind[0], last, way) + kind[1:] for kind in kinds])
+        for t in which:
+            project_mid(last, t)
+
+    def end(which, pieces, u, side_of, first=False):
+        for way in range(2):
+            need(("last", way, u, side_of))
+        for t in which:
+            for piece in pieces:
+                finalize(t, piece, first and t == which[0] and piece == pieces[0])
+
+    across_done = [0]
+
+    def take_across(count):
+        for _ in range(count):
+            serve_across(across_done[0])
+            across_done[0] += 1
+
+    def some(fn, *args, **kwargs):
+        return functools.partial(fn, *args, **kwargs)
+
+    def begun():
+        hid_load.wait()
+        close_totals()
+
+    count = len(units)
+    plan = {
+        0: [some(attend_some, count // 3)],
+        1: [some(attend_some, count // 12)],
+        2: [some(attend_some, count // 5 + 1)],
+        3: [some(attend_some, count // 5 + 1)],
+        4: [some(attend_some, count)],
+        5: [turn_left, prepare_weights, clear_halos],
+        6: [some(prepare_hot, 0), some(prepare_hot, 1)],
+        7: [prepare_totals, send_totals],
+        8: [some(first_ones, range(3))],
+        9: [some(first_ones, range(3, 6))],
+        10: [begun],
+    }
+    across_after = {4: 4}
+    for d in range(2, reach):
+        for u in range(4):
+            across_after[4 * d + u - 3] = 1
+    tail = len(slots) - 4
     for d in range(2, last):
-        at = 4 * d + 4
-        work[at] += [functools.partial(mid_ones, d, range(6))]
-
-    def third_middle():
-        mid_ones(last, (2, 3))
-
-    def end_outer():
-        for way in range(2):
-            need(("far", last, way, 0), ("last", way, 0))
-        for i, t in enumerate((0, 5)):
-            project_mid(last, t)
-            for piece in range(2):
-                finalize(t, piece, first=i == 0 and piece == 0)
-
-    def end_inner(t):
-        for way in range(2):
-            need(("far", last, way, 1), ("last", way, 1))
-        project_mid(last, t)
-        for piece in range(2):
-            finalize(t, piece)
-
-    def end_middle(piece):
-        for way in range(2):
-            need(("last", way, 2 + piece))
-        for t in (2, 3):
-            finalize(t, piece)
-
-    across_done = 0
-    for i, (d, piece) in enumerate(slots):
-        for step in work[i]:
+        at = 4 * d + 3
+        plan.setdefault(at, []).append(some(mid_ones, d, range(3)))
+        plan.setdefault(at + 1, []).append(some(mid_ones, d, range(3, 6)))
+    for i, (d, piece) in enumerate(slots[:tail]):
+        for step in plan.get(i, []):
             step()
-        if i == total_slots - 3:
-            third_middle()
-            end_outer()
-        if i == total_slots - 1:
-            end_inner(1)
         serve(d, piece)
-        until = max(0, i - 2) if i < total_slots - 3 else len(across_order)
-        if i == total_slots - 4:
-            until = i - 2 + 1
-        until = min(until, len(across_order))
-        while across_done < until:
-            serve_across(across_done)
-            across_done += 1
-    end_inner(4)
-    end_middle(0)
-    end_middle(1)
-
-    flat_one = jnp.sum(sum_one[...].T, axis=0, keepdims=True) * (1.0 / width)
+        take_across(across_after.get(i, 0))
+    third((2, 3), ("ring", 1))
+    serve(*slots[tail])
+    take_across(1)
+    third((0, 5), ("ring", 0), ("far", 0))
+    end((0,), range(2), 0, None, first=True)
+    take_across(1)
+    end((5,), range(2), 0, None)
+    serve(*slots[tail + 1])
+    serve(*slots[tail + 2])
+    third((1, 4), ("far", 1))
+    end((1,), range(2), 1, None)
+    serve(*slots[tail + 3])
+    end((4,), range(2), 1, None)
+    end((2, 3), (0,), 2, 0)
+    end((2, 3), (1,), 2, 1)
+
+    flat_one = vel[outs : outs + 1, :] * (1.0 / width)
     flat_two = jnp.sum(sum_two[...].T, axis=0, keepdims=True) * (1.0 / width)
     rate = lax.rsqrt(flat_two - flat_one * flat_one + 1e-06)
     gain = jnp.concatenate([feature[0]] * (windows * tokens // 128), axis=1)
     shift = jnp.concatenate([feature[1]] * (windows * tokens // 128), axis=1)
-    value = rate * (vel[...] - flat_one * gain) + shift
+    value = rate * (vel[:outs, :] - flat_one * gain) + shift
     weighted = []
     for q in range(PATCH * PATCH):
         cell = jnp.concatenate([cells[q]] * (C // 8), axis=0)
@@ -657,6 +694,13 @@
         send_halo(halo)
     own = [placed(alpha, 0) for alpha in range(PATCH)]
     inverse = totals[0]
+    for d, piece in slots:
+        for way in range(2):
+            ring(way, d, piece, 0).wait_send()
+    for d, piece, way in across_order:
+        yy(d, piece, way, group).wait_send()
+    for name in names:
+        part(name, core).wait_send()
     take_halo(2)
     take_halo(3)
     for alpha in range(PATCH):
@@ -665,13 +709,6 @@
         for i in range(band // LW):
             out_ref[pl.ds(PATCH * i + alpha, C, stride=BAND), :] = summed[:, i * LW : (i + 1) * LW]
 
-    for d, piece in slots:
-        for way in range(2):
-            ring(way, d, piece, 0).wait_send()
-    for d, u, way in across_order:
-        yy(d, u, way, group).wait_send()
-    for name in names:
-        part(name, core).wait_send()
     for i in range(len(halos)):
         close_halo(i)
 
@@ -706,7 +743,7 @@
             pltpu.VMEM((total, deep), bf16),
             pltpu.VMEM((total, width), f32),
             pltpu.VMEM((outs, width), bf16),
-            pltpu.VMEM((outs, width), bf16),
+            pltpu.VMEM((2 * outs + 16, width), bf16),
             pltpu.VMEM(modulation.shape, f32),
             pltpu.VMEM(anchors.shape, jnp.int32),
             pltpu.VMEM(blend_weight.shape, jnp.int32),
@@ -717,20 +754,19 @@
             pltpu.VMEM((8, band), f32),
             pltpu.VMEM((total, 128), f32),
             pltpu.VMEM((total, 128), f32),
-            pltpu.VMEM((total, 128), f32),
-            pltpu.VMEM((outs, total), f32),
+            pltpu.VMEM((outs + 16, total), f32),
             pltpu.VMEM((2, outs, 128), f32),
             pltpu.VMEM((PATCH * C, band), f32),
             pltpu.VMEM((PATCH * C, band), f32),
             pltpu.VMEM((PATCH * C, band), f32),
             pltpu.VMEM((PATCH * C, band), f32),
             dma((6 + 2 * windows,)),
-            dma((reach, 4)),
-            dma((reach, 4)),
-            dma((reach, 4)),
-            dma((reach, 4)),
-            dma((4 * (reach - 1),)),
-            dma((4 * (reach - 1),)),
+            dma((reach, 5)),
+            dma((reach, 5)),
+            dma((reach, 5)),
+            dma((reach, 5)),
+            dma((6 * (reach - 1),)),
+            dma((6 * (reach - 1),)),
             dma((parts,)),
             dma((parts,)),
             dma((4,)),

time: 50.8 us -> 47.2 us (0.929)
  Pallas kernels: 49.1 us -> 45.5 us
    pallas_call x1, Pallas kernels: 49.1 us -> 45.5 us  [shards(): pl.pallas_call(functools.partial(block_kernel, n), out_shape=jax.ShapeDty...]
where the time goes in v2:
time: 47.2 us; the launch traced here: 47 us
  Pallas kernels  45.5 us (96%)
  local copies, waits for them, and re-layouts  1.57 us (3%)
    pallas_call x1, Pallas kernels, shards(): pl.pallas_call(functools.partial(block_kernel, n), out_shape=jax.ShapeDty...  45.5 us
    unnamed x1, local copies, waits for them, and re-layouts  1.57 us

profile of v2, /device:TPU:8, one launch (start us, length us, event | category | flops | bytes accessed | tf_op | source)
XLA Modules:
  0.0 47.0 jit_solution(13981772901012656173)
XLA Ops:
  0.0 45.5 %shard_map.82 = f32[256,64]{1,0:T(8,128)} custom-call(bf16[2,256,4608]{2,1,0:T(8,128)(2,1)} %qkv_hbm.1, bf16[2,128,3072]{2,1,0:T(8,128)(2,1)} %txt_hbm.1, bf16[512,3072]{1,0:T(8,128)(2,1)} %bitcast.3, bf16[96,3072]{1,0:T(8,128)(2,1)} %wp_hbm.1, bf16[64,3072]{1,0:T(8,128)(2,1)} %bitcast.5, f32[3,3072]{1,0:T(4,128)} %mod_hbm.1, s32[2,2]{1,0:T(2,128)} %anchors_hbm.1, ...), custom_call_target="tpu_custom_call" | custom-call | tf_op jit(solution)/shard_map/pallas_call | solution.py:730
  45.5 1.6 %copy.10 = f32[16,16,64]{2,1,0:T(8,128)} copy(f32[16,16,64]{2,1,0:T(8,128)} %bitcast.4) | data formatting | bytes 131072

commit v3 on v2

--- a/solution.py
+++ b/solution.py
@@ -146,13 +146,9 @@
     near_in,
     far_in,
     load_sems,
-    cw_send,
-    cw_recv,
-    ccw_send,
-    ccw_recv,
-    y_send,
+    sent,
+    ring_recv,
     y_recv,
-    part_send,
     part_recv,
     halo_send,
     halo_recv,
@@ -204,64 +200,89 @@
     def cut(way, which, piece):
         u, side_of = piece
         col = column(way, which, u)
-        return (col, unit) if side_of is None else (col + side_of * half, half)
-
-    def mark(piece):
-        return 4 if piece[1] == 1 else piece[0]
+        if side_of is None:
+            return col, unit
+        return col + (way if side_of == 2 else side_of) * half, half
+
+    pair = (2, 2)
+
+    whole = [(u, None) for u in range(4)]
+    closing = [pair, (0, None), (1, 0), (1, 1)]
+    slots = [(1, (0, 0)), (1, (0, 1)), (1, (1, None)), (1, (2, None)), (1, (3, None))]
+    slots += [(d, piece) for d in range(2, reach) for piece in whole]
+    slots += [(reach, piece) for piece in closing]
+    last = reach - 1
+    across_groups = [[(1, (0, side_of), way) for side_of in range(2) for way in range(2)]]
+    across_groups += [
+        [(d, piece, way) for way in range(2)]
+        for d in range(1, last)
+        for piece in whole[:2]
+        if (d, piece[0]) != (1, 0)
+    ]
+    across_groups += [[(last, piece, way)] for piece in whole[:2] for way in range(2)]
+    across_groups += [[(reach, pair, way)] for way in range(2)]
+    across_of = {copy: i for i, group_of in enumerate(across_groups) for copy in group_of}
+
+    def block_of(d, pieces, crossed, ways=(0, 1)):
+        found = [("ring", d, way, piece) for way in ways for piece in pieces]
+        return found + [("far", d, way, piece) for way in ways for piece in crossed]
+
+    part_groups = {"own": [("own",)], "first": block_of(1, whole, whole[:2])}
+    for d in range(2, last):
+        for u in range(2):
+            part_groups["mid", d, u] = block_of(d, whole[u : u + 1], whole[u : u + 1])
+        part_groups["mid", d, 2] = block_of(d, whole[2:], [])
+    part_groups["inner"] = block_of(last, whole[2:], [])
+    for u in range(2):
+        for way in range(2):
+            part_groups["outer", u, way] = [
+                ("ring", last, 1 - way, whole[u]),
+                ("far", last, way, whole[u]),
+            ]
+    part_groups["pair"] = block_of(reach, [pair], [])
+    part_groups["end"] = block_of(reach, [(0, None)], [])
+    for side_of in range(2):
+        part_groups["close", side_of] = block_of(reach, [(1, side_of)], []) + [
+            ("far", reach, side_of, pair)
+        ]
+    part_of = {name: i for i, held in enumerate(part_groups.values()) for name in held}
 
     def ring(way, d, piece, hop):
         ref = region(source(way, d - 1 + hop), core, *cut(way, group, piece))
-        send, recv = (ccw_send, ccw_recv) if way else (cw_send, cw_recv)
-        i = mark(piece)
-        return remote(ref, ref, send.at[d - 1, i], recv.at[d - 1, i], backward if way else onward)
+        arrived = ring_recv.at[slots.index((d, piece))]
+        return remote(ref, ref, sent.at[0], arrived, backward if way else onward)
 
     def yy(d, piece, way, which):
         ref = region(source(way, d), core, *cut(way, which, piece))
-        i = mark(piece)
-        if i == 4:
-            i = 2
-        j = ((d - 1) * 3 + i) * 2 + way
-        return remote(ref, ref, y_send.at[j], y_recv.at[j], across)
-
-    names = [("own",)]
-    for d in range(1, reach):
-        for way in range(2):
-            names += [("ring", d, way, 0), ("ring", d, way, 1)]
-            names += [("far", d, way, 0), ("far", d, way, 1)] if d == reach - 1 else [("both", d, way)]
-    for way in range(2):
-        names += [("last", way, 0, None), ("last", way, 1, None)]
-        names += [("last", way, 2, 0), ("last", way, 2, 1)]
-    spot_of = {name: i for i, name in enumerate(names)}
-
-    def part(name, which_core):
-        kind = name[0]
-        if kind == "own":
-            ref = region(chip, which_core, 0, width)
-        elif kind == "ring":
-            _, d, way, upper = name
-            low = jnp.minimum(column(way, group, 0), column(way, group, 1))
-            col = 2 * unit if upper else low
-            ref = region(source(way, d), which_core, col, 2 * unit)
-        elif kind == "both":
-            _, d, way = name
-            low = jnp.minimum(column(way, 1 - group, 0), column(way, 1 - group, 1))
-            ref = region(source(way, d), which_core, low, 2 * unit)
-        elif kind == "far":
-            _, d, way, u = name
-            ref = region(source(way, d), which_core, column(way, 1 - group, u), unit)
+        return remote(ref, ref, sent.at[0], y_recv.at[across_of[d, piece, way]], across)
+
+    def part(name):
+        if name[0] == "own":
+            ref = region(chip, core, 0, width)
         else:
-            _, way, u, side_of = name
-            ref = region(source(way, reach), which_core, *cut(way, group, (u, side_of)))
-        i = spot_of[name]
-        return remote(ref, ref, part_send.at[i], part_recv.at[i], partner)
+            kind, d, way, piece = name
+            which = group if kind == "ring" else 1 - group
+            ref = region(source(way, d), core, *cut(way, which, piece))
+        return remote(ref, ref, sent.at[0], part_recv.at[part_of[name]], partner)
+
+    def arrived(sem, halves):
+        if halves % 2:
+            ref = weights.at[pl.ds(0, halves * rows), pl.ds(0, half)]
+        else:
+            ref = weights.at[pl.ds(0, halves // 2 * rows), pl.ds(0, unit)]
+        pltpu.make_async_copy(ref, ref, sem).wait()
+
+    def size_of(piece):
+        return 2 if piece[1] is None else 1
 
     landed = set()
 
-    def need(*wanted):
-        for name in wanted:
-            if name not in landed:
-                landed.add(name)
-                part(name, 1 - core).wait_recv()
+    def need(name):
+        if name not in landed:
+            landed.add(name)
+            held = part_groups[name]
+            sizes = [12 if one[0] == "own" else size_of(one[3]) for one in held]
+            arrived(part_recv.at[part_of[held[0]]], sum(sizes))
 
     own_load = pltpu.make_async_copy(wp_hbm, region(chip, core, 0, width), load_sems.at[0])
     own_load.start()
@@ -302,15 +323,12 @@
     pl.semaphore_wait(barrier, expected)
 
     own_load.wait()
-    slots = [(1, (0, 0)), (1, (0, 1)), (1, (1, None)), (1, (2, None)), (1, (3, None))]
-    slots += [(d, (u, None)) for d in range(2, reach) for u in range(4)]
-    slots += [(reach, (0, None)), (reach, (1, None)), (reach, (2, 0)), (reach, (2, 1))]
     for d, piece in slots[:5]:
         ring(0, d, piece, 0).start()
         ring(1, d, piece, 0).start()
-    part(("own",), core).start()
-    for pair in loads[1:]:
-        for copy in pair:
+    part(("own",)).start()
+    for both in loads[1:]:
+        for copy in both:
             copy.start()
     for copy in side_loads:
         copy.start()
@@ -361,8 +379,8 @@
         held = [chip, source(0, 1), source(1, 1)]
         acc[:, at] = jnp.dot(left_first[...], right(held, at), preferred_element_type=jnp.float32)
 
-    def project_mid(d, t):
-        at = pl.ds(t * unit, unit)
+    def project_mid(d, col):
+        at = pl.ds(pl.multiple_of(col, 128), unit)
         held = [source(0, d), source(1, d)]
         term = jnp.dot(left_mid[d - 2], right(held, at), preferred_element_type=jnp.float32)
         if d == 2:
@@ -370,8 +388,8 @@
         else:
             acc[:, at] += mod[0:1, at] * term
 
-    def finalize(t, piece, first=False):
-        at = pl.ds(t * unit + piece * half, half)
+    def finalize(col, first=False):
+        at = pl.ds(pl.multiple_of(col, 128), half)
         term = jnp.dot(
             left_last[...], right([source(0, reach)], at), preferred_element_type=jnp.float32
         )
@@ -393,6 +411,7 @@
     grid_log = GRID.bit_length() - 1
     spread = hot.shape[2]
     band = spread // 3
+    quarters = band // 128
 
     def parity(w):
         row_at = anchors[w : w + 1, 0:1] - me * BAND
@@ -463,10 +482,15 @@
                     left, hot[alpha * PATCH + b], preferred_element_type=jnp.float32
                 )
             found.append(total)
-        upper = lax.broadcasted_iota(jnp.int32, (8, spread), 0) < 4
-        total = jnp.where(upper, found[0], found[1])
+        line = lax.broadcasted_iota(jnp.int32, (8, 128), 0)
         for i in range(3):
-            totals[i] = total[:, i * band : (i + 1) * band]
+            total = jnp.zeros((8, 128), jnp.float32)
+            for alpha in range(PATCH):
+                for q in range(quarters):
+                    at = i * band + q * 128
+                    mine = found[alpha][:, at : at + 128]
+                    total = jnp.where(line == alpha * quarters + q, mine, total)
+            totals[i] = total
 
     halos = (
         (1, remote(totals.at[1], total_near, halo_send.at[0], halo_recv.at[0], after[0])),
@@ -517,42 +541,35 @@
         summed = totals[0] + total_near[...] + total_far[...]
         totals[0] = 1.0 / jnp.maximum(summed, 1.0)
 
-    across_order = [(1, (0, 0), 0), (1, (0, 0), 1), (1, (0, 1), 0), (1, (0, 1), 1)]
-    across_order += [
-        (d, (u, None), way)
-        for d in range(1, reach)
-        for u in range(2)
-        for way in range(2)
-        if (d, u) != (1, 0)
-    ]
+    def hand(kind, d, way, piece):
+        if (d, piece[0]) == (1, 0):
+            if piece[1] == 0:
+                return
+            piece = (0, None)
+        part((kind, d, way, piece)).start()
 
     def serve(d, piece):
         u, side_of = piece
+        arrived(ring_recv.at[slots.index((d, piece))], 2 * size_of(piece))
         for way in range(2):
-            ring(way, d, piece, 1).wait_recv()
-            if d == 1 and u == 0:
-                if side_of == 1:
-                    ring(way, 2, (0, None), 0).start()
-            elif d + 1 < reach or (d + 1 == reach and u < 2):
-                ring(way, d + 1, piece, 0).start()
+            if d + 1 < reach:
+                if side_of is None:
+                    ring(way, d + 1, piece, 0).start()
+                elif side_of == 1:
+                    ring(way, d + 1, (0, None), 0).start()
             elif d + 1 == reach and u == 2:
-                ring(way, reach, (2, 0), 0).start()
-                ring(way, reach, (2, 1), 0).start()
-            if d < reach and u < 2:
+                for later in closing:
+                    ring(way, reach, later, 0).start()
+            if (d < reach and u < 2) or piece == pair:
                 yy(d, piece, way, group).start()
         for way in range(2):
-            if d < reach and u % 2 == 1:
-                part(("ring", d, way, u // 2), core).start()
-            elif d == reach:
-                part(("last", way, u, side_of), core).start()
+            hand("ring", d, way, piece)
 
     def serve_across(j):
-        d, (u, side_of), way = across_order[j]
-        yy(d, (u, side_of), way, 1 - group).wait_recv()
-        if d == reach - 1:
-            part(("far", d, way, u), core).start()
-        elif u == 1:
-            part(("both", d, way), core).start()
+        held = across_groups[j]
+        arrived(y_recv.at[j], sum(size_of(piece) for _, piece, _ in held))
+        for d, piece, way in held:
+            hand("far", d, way, piece)
 
     units = [(w, h) for w in range(windows) for h in range(HEADS)]
     ready = set()
@@ -567,34 +584,40 @@
             attend(w, h)
 
     def first_ones(which):
-        need(("own",))
-        for way in range(2):
-            need(("ring", 1, way, 0), ("ring", 1, way, 1), ("both", 1, way))
+        need("own")
+        need("first")
         for t in which:
             project_first(t)
 
-    def mid_ones(d, which):
+    def mid_ones(d, u):
+        need(("mid", d, u))
+        for t in (u, 5 - u):
+            project_mid(d, t * unit)
+
+    def third_inner():
+        need("inner")
+        for t in (2, 3):
+            project_mid(last, t * unit)
+
+    def third_outer(u, way):
+        need(("outer", u, way))
+        project_mid(last, column(way, 1 - group, u))
+
+    def end_pair():
+        need("pair")
         for way in range(2):
-            need(("ring", d, way, 0), ("ring", d, way, 1))
-            if d < reach - 1:
-                need(("both", d, way))
-        for t in which:
-            project_mid(d, t)
-
-    last = reach - 1
-
-    def third(which, *kinds):
-        for way in range(2):
-            need(*[(kind[0], last, way) + kind[1:] for kind in kinds])
-        for t in which:
-            project_mid(last, t)
-
-    def end(which, pieces, u, side_of, first=False):
-        for way in range(2):
-            need(("last", way, u, side_of))
-        for t in which:
-            for piece in pieces:
-                finalize(t, piece, first and t == which[0] and piece == pieces[0])
+            finalize(cut(way, group, pair)[0], first=way == 0)
+
+    def end(cols):
+        need("end")
+        for col in cols:
+            finalize(col)
+
+    def close(side_of):
+        need(("close", side_of))
+        for col in (unit, 4 * unit):
+            finalize(col + side_of * half)
+        finalize(cut(side_of, 1 - group, pair)[0])
 
     across_done = [0]
 
@@ -606,53 +629,52 @@
     def some(fn, *args, **kwargs):
         return functools.partial(fn, *args, **kwargs)
 
-    def begun():
-        hid_load.wait()
-        close_totals()
-
     count = len(units)
     plan = {
-        0: [some(attend_some, count // 3)],
+        0: [some(attend_some, count // 3 - 1)],
         1: [some(attend_some, count // 12)],
         2: [some(attend_some, count // 5 + 1)],
         3: [some(attend_some, count // 5 + 1)],
-        4: [some(attend_some, count)],
-        5: [turn_left, prepare_weights, clear_halos],
+        4: [some(attend_some, count // 5 + 1)],
+        5: [some(attend_some, count), turn_left, prepare_weights, clear_halos],
         6: [some(prepare_hot, 0), some(prepare_hot, 1)],
         7: [prepare_totals, send_totals],
         8: [some(first_ones, range(3))],
         9: [some(first_ones, range(3, 6))],
-        10: [begun],
+        10: [hid_load.wait],
     }
-    across_after = {4: 4}
-    for d in range(2, reach):
-        for u in range(4):
-            across_after[4 * d + u - 3] = 1
+    across_after = {4: 1, 6: 1}
+    for d in range(2, last):
+        plan.setdefault(4 * d + 2, []).extend([some(mid_ones, d, 2), some(mid_ones, d, 0)])
+        plan.setdefault(4 * d + 3, []).append(some(mid_ones, d, 1))
+        across_after[4 * d] = 1
+        across_after[4 * d + 2] = 1
     tail = len(slots) - 4
-    for d in range(2, last):
-        at = 4 * d + 3
-        plan.setdefault(at, []).append(some(mid_ones, d, range(3)))
-        plan.setdefault(at + 1, []).append(some(mid_ones, d, range(3, 6)))
-    for i, (d, piece) in enumerate(slots[:tail]):
+    across_after[tail - 2] = 1
+    across_after[tail - 1] = 1
+    across_after[tail] = 1
+    plan.setdefault(tail - 1, []).append(some(third_outer, 0, 0))
+    for i, (d, piece) in enumerate(slots[: tail + 1]):
         for step in plan.get(i, []):
             step()
         serve(d, piece)
         take_across(across_after.get(i, 0))
-    third((2, 3), ("ring", 1))
-    serve(*slots[tail])
+    third_inner()
+    third_outer(0, 1)
+    end_pair()
+    serve(*slots[tail + 1])
     take_across(1)
-    third((0, 5), ("ring", 0), ("far", 0))
-    end((0,), range(2), 0, None, first=True)
+    third_outer(1, 0)
+    close_totals()
+    serve(*slots[tail + 2])
     take_across(1)
-    end((5,), range(2), 0, None)
-    serve(*slots[tail + 1])
-    serve(*slots[tail + 2])
-    third((1, 4), ("far", 1))
-    end((1,), range(2), 1, None)
+    third_outer(1, 1)
+    end([0])
     serve(*slots[tail + 3])
-    end((4,), range(2), 1, None)
-    end((2, 3), (0,), 2, 0)
-    end((2, 3), (1,), 2, 1)
+    take_across(1)
+    end([half, 5 * unit, 5 * unit + half])
+    close(0)
+    close(1)
 
     flat_one = vel[outs : outs + 1, :] * (1.0 / width)
     flat_two = jnp.sum(sum_two[...].T, axis=0, keepdims=True) * (1.0 / width)
@@ -690,22 +712,20 @@
 
     for which, ref, halo in ((2, far_out, 3), (1, near_out, 2)):
         for alpha in range(PATCH):
-            ref[alpha * C : (alpha + 1) * C, :] = placed(alpha, which)
+            ref[alpha * C : (alpha + 1) * C, :] = placed(alpha, which).astype(jnp.bfloat16)
         send_halo(halo)
     own = [placed(alpha, 0) for alpha in range(PATCH)]
     inverse = totals[0]
-    for d, piece in slots:
-        for way in range(2):
-            ring(way, d, piece, 0).wait_send()
-    for d, piece, way in across_order:
-        yy(d, piece, way, group).wait_send()
-    for name in names:
-        part(name, core).wait_send()
+    everything = weights.at[pl.ds(0, (n - 1) * rows), :]
+    pltpu.make_async_copy(everything, everything, sent.at[0]).wait()
     take_halo(2)
     take_halo(3)
     for alpha in range(PATCH):
         at = slice(alpha * C, (alpha + 1) * C)
-        summed = (own[alpha] + near_in[at, :] + far_in[at, :]) * inverse[4 * alpha : 4 * alpha + 1, :]
+        lines = range(alpha * quarters, (alpha + 1) * quarters)
+        factor = jnp.concatenate([inverse[q : q + 1, :] for q in lines], axis=1)
+        near = near_in[at, :].astype(jnp.float32)
+        summed = (own[alpha] + near + far_in[at, :].astype(jnp.float32)) * factor
         for i in range(band // LW):
             out_ref[pl.ds(PATCH * i + alpha, C, stride=BAND), :] = summed[:, i * LW : (i + 1) * LW]
 
@@ -726,10 +746,9 @@
     vmem = pl.BlockSpec(memory_space=pltpu.VMEM)
     dma = pltpu.SemaphoreType.DMA
     f32, bf16 = jnp.float32, jnp.bfloat16
-    parts = 1 + 6 * (reach - 2) + 8 + 8
     velocity = pl.pallas_call(
         functools.partial(block_kernel, n),
-        out_shape=jax.ShapeDtypeStruct((C * BAND, LW), f32),
+        out_shape=pltpu.VMEM((C * BAND, LW), f32),
         in_specs=[any_space] * 8,
         out_specs=vmem,
         scratch_shapes=[
@@ -749,26 +768,22 @@
             pltpu.VMEM(blend_weight.shape, jnp.int32),
             pltpu.VMEM((PATCH * PATCH, 8, total), f32),
             pltpu.VMEM((PATCH * PATCH, total, spread), bf16),
-            pltpu.VMEM((3, 8, band), f32),
-            pltpu.VMEM((8, band), f32),
-            pltpu.VMEM((8, band), f32),
+            pltpu.VMEM((3, 8, 128), f32),
+            pltpu.VMEM((8, 128), f32),
+            pltpu.VMEM((8, 128), f32),
             pltpu.VMEM((total, 128), f32),
             pltpu.VMEM((total, 128), f32),
             pltpu.VMEM((outs + 16, total), f32),
             pltpu.VMEM((2, outs, 128), f32),
-            pltpu.VMEM((PATCH * C, band), f32),
-            pltpu.VMEM((PATCH * C, band), f32),
-            pltpu.VMEM((PATCH * C, band), f32),
-            pltpu.VMEM((PATCH * C, band), f32),
+            pltpu.VMEM((PATCH * C, band), bf16),
+            pltpu.VMEM((PATCH * C, band), bf16),
+            pltpu.VMEM((PATCH * C, band), bf16),
+            pltpu.VMEM((PATCH * C, band), bf16),
             dma((6 + 2 * windows,)),
-            dma((reach, 5)),
-            dma((reach, 5)),
-            dma((reach, 5)),
-            dma((reach, 5)),
-            dma((6 * (reach - 1),)),
-            dma((6 * (reach - 1),)),
-            dma((parts,)),
-            dma((parts,)),
+            dma((1,)),
+            dma((4 * reach + 1,)),
+            dma((2 * (reach - 2) + 6,)),
+            dma((3 * (reach - 3) + 11,)),
             dma((4,)),
             dma((4,)),
         ],

time: 47.2 us -> 43.8 us (0.928)
  Pallas kernels: 45.5 us -> 43 us
  local copies, waits for them, and re-layouts: 1.57 us -> 0.66 us
    pallas_call x1, Pallas kernels: 45.5 us -> 43 us  [shards(): pl.pallas_call(functools.partial(block_kernel, n), out_shape=pltpu.VMEM((...]
    unnamed x1, local copies, waits for them, and re-layouts: 1.57 us -> 0.66 us
where the time goes in v3:
time: 43.8 us; the launch traced here: 43.6 us
  Pallas kernels  43 us (98%)
  local copies, waits for them, and re-layouts  0.66 us (2%)
    pallas_call x1, Pallas kernels, shards(): pl.pallas_call(functools.partial(block_kernel, n), out_shape=pltpu.VMEM((...  43 us

profile of v3, /device:TPU:8, one launch (start us, length us, event | category | flops | bytes accessed | tf_op | source)
XLA Modules:
  0.0 43.6 jit_solution(10943699920505664825)
XLA Ops:
  0.0 43.0 %shard_map.82 = f32[256,64]{1,0:T(8,128)S(1)} custom-call(bf16[2,256,4608]{2,1,0:T(8,128)(2,1)} %qkv_hbm.1, bf16[2,128,3072]{2,1,0:T(8,128)(2,1)} %txt_hbm.1, bf16[512,3072]{1,0:T(8,128)(2,1)} %bitcast.4, bf16[96,3072]{1,0:T(8,128)(2,1)} %wp_hbm.1, bf16[64,3072]{1,0:T(8,128)(2,1)} %bitcast.5, f32[3,3072]{1,0:T(4,128)} %mod_hbm.1, s32[2,2]{1,0:T(2,128)} %anchors_hbm.1, ...), custom_call_target="tpu_custom_call" | custom-call | tf_op jit(solution)/shard_map/pallas_call | solution.py:749
  43.0 0.7 %copy.10 = f32[16,16,64]{2,1,0:T(8,128)} copy(f32[16,16,64]{2,1,0:T(8,128)S(1)} %bitcast.3) | data formatting | bytes 131072

commit v4 on v3

--- a/solution.py
+++ b/solution.py
@@ -125,6 +125,8 @@
     att,
     left_first,
     left_mid,
+    left_side,
+    left_close,
     left_last,
     acc,
     wout,
@@ -183,6 +185,9 @@
     def source(way, d):
         return chip_at(place + d) if way else chip_at(place - d)
 
+    def toward(way, d):
+        return chip_at(place + (2 * way - 1) * d)
+
     def column(way, which, u):
         flip = which * (5 - 2 * u) * unit
         return (5 - u) * unit - flip if way else u * unit + flip
@@ -202,25 +207,20 @@
         col = column(way, which, u)
         if side_of is None:
             return col, unit
-        return col + (way if side_of == 2 else side_of) * half, half
-
-    pair = (2, 2)
+        return col + side_of * half, half
 
     whole = [(u, None) for u in range(4)]
-    closing = [pair, (0, None), (1, 0), (1, 1)]
-    slots = [(1, (0, 0)), (1, (0, 1)), (1, (1, None)), (1, (2, None)), (1, (3, None))]
-    slots += [(d, piece) for d in range(2, reach) for piece in whole]
-    slots += [(reach, piece) for piece in closing]
+    opening = [(0, 0), (0, 1)]
+    slots = [(d, piece) for d in range(1, reach) for piece in opening + whole[1:]]
+    slots += [(reach, piece) for piece in whole[:2]]
     last = reach - 1
-    across_groups = [[(1, (0, side_of), way) for side_of in range(2) for way in range(2)]]
-    across_groups += [
-        [(d, piece, way) for way in range(2)]
-        for d in range(1, last)
-        for piece in whole[:2]
-        if (d, piece[0]) != (1, 0)
-    ]
-    across_groups += [[(last, piece, way)] for piece in whole[:2] for way in range(2)]
-    across_groups += [[(reach, pair, way)] for way in range(2)]
+    across_groups = []
+    for d in range(1, reach):
+        across_groups.append([(d, piece, way) for piece in opening for way in range(2)])
+        if d < last:
+            across_groups.append([(d, whole[1], way) for way in range(2)])
+        else:
+            across_groups += [[(d, whole[1], way)] for way in range(2)]
     across_of = {copy: i for i, group_of in enumerate(across_groups) for copy in group_of}
 
     def block_of(d, pieces, crossed, ways=(0, 1)):
@@ -232,38 +232,44 @@
         for u in range(2):
             part_groups["mid", d, u] = block_of(d, whole[u : u + 1], whole[u : u + 1])
         part_groups["mid", d, 2] = block_of(d, whole[2:], [])
-    part_groups["inner"] = block_of(last, whole[2:], [])
+    for u in range(4):
+        part_groups["ring", u] = block_of(last, whole[u : u + 1], [])
     for u in range(2):
-        for way in range(2):
-            part_groups["outer", u, way] = [
-                ("ring", last, 1 - way, whole[u]),
-                ("far", last, way, whole[u]),
-            ]
-    part_groups["pair"] = block_of(reach, [pair], [])
-    part_groups["end"] = block_of(reach, [(0, None)], [])
-    for side_of in range(2):
-        part_groups["close", side_of] = block_of(reach, [(1, side_of)], []) + [
-            ("far", reach, side_of, pair)
-        ]
+        part_groups["far", u] = block_of(last, [], whole[u : u + 1])
+    for u in range(2):
+        part_groups["end", u] = block_of(reach, whole[u : u + 1], [])
     part_of = {name: i for i, held in enumerate(part_groups.values()) for name in held}
 
     def ring(way, d, piece, hop):
         ref = region(source(way, d - 1 + hop), core, *cut(way, group, piece))
-        arrived = ring_recv.at[slots.index((d, piece))]
-        return remote(ref, ref, sent.at[0], arrived, backward if way else onward)
+        there = ring_recv.at[slots.index((d, piece))]
+        return remote(ref, ref, sent.at[d // reach], there, backward if way else onward)
+
+    def final_ring(way, side_of, which_core):
+        ref = region(source(way, last), which_core, *cut(way, group, (2, side_of)))
+        there = ring_recv.at[len(slots) + side_of]
+        return remote(ref, ref, sent.at[1], there, backward if way else onward)
+
+    def final_part(way, side_of):
+        col, cols = cut(way, group, (2, side_of))
+        row = pl.multiple_of(source(way, reach) * deep, 16)
+        ref = weights.at[pl.ds(row, deep), pl.ds(pl.multiple_of(col, 128), cols)]
+        there = part_recv.at[len(part_groups) + side_of]
+        return remote(ref, ref, sent.at[1], there, partner)
 
     def yy(d, piece, way, which):
         ref = region(source(way, d), core, *cut(way, which, piece))
         return remote(ref, ref, sent.at[0], y_recv.at[across_of[d, piece, way]], across)
 
     def part(name):
+        d = 0
         if name[0] == "own":
             ref = region(chip, core, 0, width)
         else:
             kind, d, way, piece = name
             which = group if kind == "ring" else 1 - group
             ref = region(source(way, d), core, *cut(way, which, piece))
-        return remote(ref, ref, sent.at[0], part_recv.at[part_of[name]], partner)
+        return remote(ref, ref, sent.at[d // reach], part_recv.at[part_of[name]], partner)
 
     def arrived(sem, halves):
         if halves % 2:
@@ -277,12 +283,21 @@
 
     landed = set()
 
+    def wait_part(name):
+        held = part_groups[name]
+        sizes = [12 if one[0] == "own" else size_of(one[3]) for one in held]
+        arrived(part_recv.at[part_of[held[0]]], sum(sizes))
+
     def need(name):
         if name not in landed:
             landed.add(name)
-            held = part_groups[name]
-            sizes = [12 if one[0] == "own" else size_of(one[3]) for one in held]
-            arrived(part_recv.at[part_of[held[0]]], sum(sizes))
+            wait_part(name)
+
+    def only(which_core, *steps):
+        @pl.when(core == which_core)
+        def _():
+            for step in steps:
+                step()
 
     own_load = pltpu.make_async_copy(wp_hbm, region(chip, core, 0, width), load_sems.at[0])
     own_load.start()
@@ -363,13 +378,16 @@
         return pl.ds(pl.multiple_of(which_chip * deep, 16), deep)
 
     def turn_left():
-        def turned(chips_held):
+        def joined(chips_held):
             return jnp.concatenate([att[spot(c), :] for c in chips_held], axis=0).T
 
-        left_first[...] = turned([chip, source(0, 1), source(1, 1)])
+        left_first[...] = joined([chip, source(0, 1), source(1, 1)])
         for d in range(2, reach):
-            left_mid[d - 2] = turned([source(0, d), source(1, d)])
-        left_last[...] = turned([source(0, reach)])
+            left_mid[d - 2] = joined([source(0, d), source(1, d)])
+        for way in range(2):
+            left_side[way] = joined([source(way, last)])
+            left_close[way] = joined([source(way, last), source(0, reach)])
+        left_last[...] = joined([source(0, reach)])
 
     def right(chips_held, at):
         return jnp.concatenate([weights[spot(c), at] for c in chips_held], axis=0)
@@ -388,22 +406,37 @@
         else:
             acc[:, at] += mod[0:1, at] * term
 
-    def finalize(col, first=False):
-        at = pl.ds(pl.multiple_of(col, 128), half)
+    def project_side(t, way):
+        at = pl.ds(t * unit, unit)
         term = jnp.dot(
-            left_last[...], right([source(0, reach)], at), preferred_element_type=jnp.float32
+            left_side[way], weights[spot(toward(way, last)), at], preferred_element_type=jnp.float32
         )
-        residual = acc[:, at] + mod[0:1, at] * term
-        if first:
-            mean = jnp.sum(residual, axis=-1, keepdims=True) * (1.0 / half)
-            centre[...] = jnp.broadcast_to(mean, centre.shape)
+        acc[:, at] += mod[0:1, at] * term
+
+    def finalize(cols, far=None, first=False):
+        spans = [pl.ds(pl.multiple_of(col, 128), half) for col in cols]
+        held = [source(0, reach)] if far is None else [toward(far, last), source(0, reach)]
+        term = jnp.dot(
+            left_last[...] if far is None else left_close[far],
+            jnp.concatenate([right(held, at) for at in spans], axis=1),
+            preferred_element_type=jnp.float32,
+        )
         lanes = centre.shape[1]
-        pieces = [residual[:, i : i + lanes] - centre[...] for i in range(0, half, lanes)]
+        pieces = []
+        for i, at in enumerate(spans):
+            residual = acc[:, at] + mod[0:1, at] * term[:, i * half : (i + 1) * half]
+            if first and i == 0:
+                mean = jnp.sum(residual, axis=-1, keepdims=True) * (1.0 / half)
+                centre[...] = jnp.broadcast_to(mean, centre.shape)
+            pieces += [residual[:, k : k + lanes] - centre[...] for k in range(0, half, lanes)]
         two = functools.reduce(lambda a, b: a + b, [x * x for x in pieces])
         sum_two[...] = two if first else sum_two[...] + two
         moved = jnp.concatenate(pieces, axis=1).astype(jnp.bfloat16)
         term = lax.dot_general(
-            wperm[:, at], moved, (((1,), (1,)), ((), ())), preferred_element_type=jnp.float32
+            jnp.concatenate([wperm[:, at] for at in spans], axis=1),
+            moved,
+            (((1,), (1,)), ((), ())),
+            preferred_element_type=jnp.float32,
         )
         term = jnp.concatenate([term[:outs] + term[outs : 2 * outs], term[2 * outs :]], axis=0)
         vel[...] = term if first else vel[...] + term
@@ -454,13 +487,21 @@
         for w in range(windows):
             odd, row_at, col_at = parity(w)
             tall = (token >> grid_log) + row_at + odd * (1 - alpha)
-            for b in range(PATCH):
-                wide = (PATCH * (token & (GRID - 1)) + b + col_at) & (LW - 1)
-                target = tall * LW + wide - lane
-                for j in range(spread // 128):
-                    hot[alpha * PATCH + b, w * tokens : (w + 1) * tokens, j * 128 : (j + 1) * 128] = (
-                        jnp.where(target == j * 128, 1.0, 0.0).astype(jnp.bfloat16)
-                    )
+            wide = (PATCH * (token & (GRID - 1)) + col_at) & (LW - 1)
+            target = tall * LW + wide - lane
+            for j in range(spread // 128):
+                hot[alpha, w * tokens : (w + 1) * tokens, j * 128 : (j + 1) * 128] = jnp.where(
+                    target == j * 128, 1.0, 0.0
+                ).astype(jnp.bfloat16)
+
+    def turned(field):
+        lane = lax.broadcasted_iota(jnp.int32, (field.shape[0], 128), 1) & (LW - 1)
+        moved = []
+        for j in range(0, field.shape[1], 128):
+            piece = field[:, j : j + 128]
+            step, wrap = pltpu.roll(piece, 1, 1), pltpu.roll(piece, 1 + LW, 1)
+            moved.append(jnp.where(lane == 0, wrap, step))
+        return jnp.concatenate(moved, axis=1)
 
     def by_parity(w, straight, swapped):
         odd = parity(w)[0]
@@ -469,7 +510,7 @@
     def prepare_totals():
         found = []
         for alpha in range(PATCH):
-            total = jnp.zeros((8, spread), jnp.float32)
+            sides = []
             for b in range(PATCH):
                 held = []
                 for w in range(windows):
@@ -477,11 +518,10 @@
                     straight = cells[alpha * PATCH + b, :, at]
                     swapped = cells[(1 - alpha) * PATCH + b, :, at]
                     held.append(by_parity(w, straight, swapped))
-                left = jnp.concatenate(held, axis=1).astype(jnp.bfloat16)
-                total += jnp.dot(
-                    left, hot[alpha * PATCH + b], preferred_element_type=jnp.float32
-                )
-            found.append(total)
+                sides.append(jnp.concatenate(held, axis=1))
+            left = jnp.concatenate(sides, axis=0).astype(jnp.bfloat16)
+            total = jnp.dot(left, hot[alpha], preferred_element_type=jnp.float32)
+            found.append(total[:8] + turned(total[8:]))
         line = lax.broadcasted_iota(jnp.int32, (8, 128), 0)
         for i in range(3):
             total = jnp.zeros((8, 128), jnp.float32)
@@ -542,28 +582,50 @@
         totals[0] = 1.0 / jnp.maximum(summed, 1.0)
 
     def hand(kind, d, way, piece):
-        if (d, piece[0]) == (1, 0):
-            if piece[1] == 0:
-                return
-            piece = (0, None)
+        if piece == opening[0]:
+            return
+        if piece == opening[1]:
+            piece = whole[0]
         part((kind, d, way, piece)).start()
 
     def serve(d, piece):
-        u, side_of = piece
+        u = piece[0]
         arrived(ring_recv.at[slots.index((d, piece))], 2 * size_of(piece))
         for way in range(2):
             if d + 1 < reach:
-                if side_of is None:
-                    ring(way, d + 1, piece, 0).start()
-                elif side_of == 1:
-                    ring(way, d + 1, (0, None), 0).start()
-            elif d + 1 == reach and u == 2:
-                for later in closing:
-                    ring(way, reach, later, 0).start()
-            if (d < reach and u < 2) or piece == pair:
+                ring(way, d + 1, piece, 0).start()
+            elif d == last and piece == opening[1]:
+                ring(way, reach, whole[0], 0).start()
+            elif d == last and u == 1:
+                ring(way, reach, whole[1], 0).start()
+            if d < reach and u < 2:
                 yy(d, piece, way, group).start()
+        if d == last and u == 2:
+
+            @pl.when(core == 1)
+            def _():
+                for way in range(2):
+                    final_ring(way, 0, 1).start()
+
         for way in range(2):
             hand("ring", d, way, piece)
+
+    def send_final():
+        need(("ring", 2))
+
+        @pl.when(core == 1)
+        def _():
+            for side_of, which_core in ((0, 0), (1, 1), (1, 0)):
+                for way in range(2):
+                    final_ring(way, side_of, which_core).start()
+
+    def serve_final(side_of):
+        arrived(ring_recv.at[len(slots) + side_of], 4)
+        for way in range(2):
+            final_part(way, side_of).start()
+
+    def take_final(side_of):
+        arrived(part_recv.at[len(part_groups) + side_of], 4)
 
     def serve_across(j):
         held = across_groups[j]
@@ -595,29 +657,23 @@
             project_mid(d, t * unit)
 
     def third_inner():
-        need("inner")
+        wait_part(("ring", 3))
         for t in (2, 3):
             project_mid(last, t * unit)
 
-    def third_outer(u, way):
-        need(("outer", u, way))
-        project_mid(last, column(way, 1 - group, u))
-
-    def end_pair():
-        need("pair")
-        for way in range(2):
-            finalize(cut(way, group, pair)[0], first=way == 0)
-
-    def end(cols):
-        need("end")
-        for col in cols:
-            finalize(col)
+    def third_side(u):
+        need(("ring", u))
+        project_side(u, group)
+        project_side(5 - u, 1 - group)
+
+    def end(u):
+        wait_part(("far", u))
+        wait_part(("end", u))
+        for t, far in ((u, 1 - group), (5 - u, group)):
+            finalize([t * unit, t * unit + half], far, first=t == 0)
 
     def close(side_of):
-        need(("close", side_of))
-        for col in (unit, 4 * unit):
-            finalize(col + side_of * half)
-        finalize(cut(side_of, 1 - group, pair)[0])
+        finalize([t * unit + side_of * half for t in (2, 3)])
 
     across_done = [0]
 
@@ -636,44 +692,40 @@
         2: [some(attend_some, count // 5 + 1)],
         3: [some(attend_some, count // 5 + 1)],
         4: [some(attend_some, count // 5 + 1)],
-        5: [some(attend_some, count), turn_left, prepare_weights, clear_halos],
-        6: [some(prepare_hot, 0), some(prepare_hot, 1)],
-        7: [prepare_totals, send_totals],
-        8: [some(first_ones, range(3))],
-        9: [some(first_ones, range(3, 6))],
-        10: [hid_load.wait],
+        5: [some(attend_some, count), turn_left],
+        6: [prepare_weights, clear_halos],
+        7: [some(prepare_hot, 0), some(prepare_hot, 1)],
+        8: [prepare_totals, send_totals],
+        9: [some(first_ones, range(3))],
+        11: [some(first_ones, range(3, 6)), hid_load.wait],
     }
-    across_after = {4: 1, 6: 1}
+    across_after = {4: 1, 7: 1}
     for d in range(2, last):
-        plan.setdefault(4 * d + 2, []).extend([some(mid_ones, d, 2), some(mid_ones, d, 0)])
-        plan.setdefault(4 * d + 3, []).append(some(mid_ones, d, 1))
-        across_after[4 * d] = 1
-        across_after[4 * d + 2] = 1
-    tail = len(slots) - 4
-    across_after[tail - 2] = 1
+        plan.setdefault(5 * d + 2, []).extend([some(mid_ones, d, 2), some(mid_ones, d, 0)])
+        plan.setdefault(5 * d + 4, []).append(some(mid_ones, d, 1))
+        across_after[5 * d - 1] = 1
+        across_after[5 * d + 2] = 1
+    plan.setdefault(5 * last - 2, []).append(some(third_side, 0))
+    plan.setdefault(5 * last - 1, []).append(some(third_side, 1))
+    tail = len(slots) - 2
     across_after[tail - 1] = 1
-    across_after[tail] = 1
-    plan.setdefault(tail - 1, []).append(some(third_outer, 0, 0))
-    for i, (d, piece) in enumerate(slots[: tail + 1]):
+    for i, (d, piece) in enumerate(slots[:tail]):
         for step in plan.get(i, []):
             step()
         serve(d, piece)
         take_across(across_after.get(i, 0))
-    third_inner()
-    third_outer(0, 1)
-    end_pair()
+    send_final()
+    only(0, third_inner)
+    serve(*slots[tail])
+    take_across(1)
+    only(1, third_inner)
+    close_totals()
+    only(0, some(end, 0))
     serve(*slots[tail + 1])
     take_across(1)
-    third_outer(1, 0)
-    close_totals()
-    serve(*slots[tail + 2])
-    take_across(1)
-    third_outer(1, 1)
-    end([0])
-    serve(*slots[tail + 3])
-    take_across(1)
-    end([half, 5 * unit, 5 * unit + half])
-    close(0)
+    only(1, some(end, 0), some(serve_final, 0), some(close, 0), some(serve_final, 1))
+    end(1)
+    only(0, some(take_final, 0), some(close, 0), some(take_final, 1))
     close(1)
 
     flat_one = vel[outs : outs + 1, :] * (1.0 / width)
@@ -688,6 +740,7 @@
         weighted.append(value[q * C : (q + 1) * C] * cell)
     chosen = []
     for alpha in range(PATCH):
+        rows_of = []
         for b in range(PATCH):
             held = []
             for w in range(windows):
@@ -697,35 +750,35 @@
                 held.append(by_parity(w, straight, swapped))
             both = jnp.concatenate(held, axis=1)
             high = both.astype(jnp.bfloat16)
-            low = (both - high.astype(jnp.float32)).astype(jnp.bfloat16)
-            chosen.append(jnp.concatenate([high, low], axis=0))
+            rows_of += [high, (both - high.astype(jnp.float32)).astype(jnp.bfloat16)]
+        chosen.append(jnp.concatenate(rows_of, axis=0))
 
     def placed(alpha, which):
-        total = jnp.zeros((2 * C, band), jnp.float32)
-        for b in range(PATCH):
-            total += jnp.dot(
-                chosen[alpha * PATCH + b],
-                hot[alpha * PATCH + b, :, which * band : (which + 1) * band],
-                preferred_element_type=jnp.float32,
-            )
-        return total[:C] + total[C:]
+        at = slice(which * band, (which + 1) * band)
+        total = jnp.dot(chosen[alpha], hot[alpha, :, at], preferred_element_type=jnp.float32)
+        return total[:C] + total[C : 2 * C] + turned(total[2 * C : 3 * C] + total[3 * C :])
 
     for which, ref, halo in ((2, far_out, 3), (1, near_out, 2)):
         for alpha in range(PATCH):
-            ref[alpha * C : (alpha + 1) * C, :] = placed(alpha, which).astype(jnp.bfloat16)
+            ref[alpha * C : (alpha + 1) * C, :] = placed(alpha, which).astype(ref.dtype)
         send_halo(halo)
     own = [placed(alpha, 0) for alpha in range(PATCH)]
     inverse = totals[0]
-    everything = weights.at[pl.ds(0, (n - 1) * rows), :]
+    everything = weights.at[pl.ds(0, (4 * reach - 3) * rows), :]
     pltpu.make_async_copy(everything, everything, sent.at[0]).wait()
+    for side_of in range(2):
+
+        @pl.when(core == side_of)
+        def _():
+            arrived(sent.at[1], 16 * (1 + side_of))
+
     take_halo(2)
     take_halo(3)
     for alpha in range(PATCH):
         at = slice(alpha * C, (alpha + 1) * C)
         lines = range(alpha * quarters, (alpha + 1) * quarters)
         factor = jnp.concatenate([inverse[q : q + 1, :] for q in lines], axis=1)
-        near = near_in[at, :].astype(jnp.float32)
-        summed = (own[alpha] + near + far_in[at, :].astype(jnp.float32)) * factor
+        summed = (own[alpha] + near_in[at, :] + far_in[at, :].astype(jnp.float32)) * factor
         for i in range(band // LW):
             out_ref[pl.ds(PATCH * i + alpha, C, stride=BAND), :] = summed[:, i * LW : (i + 1) * LW]
 
@@ -759,6 +812,8 @@
             pltpu.VMEM((n * rows, total), bf16),
             pltpu.VMEM((total, 3 * deep), bf16),
             pltpu.VMEM((reach - 2, total, 2 * deep), bf16),
+            pltpu.VMEM((2, total, deep), bf16),
+            pltpu.VMEM((2, total, 2 * deep), bf16),
             pltpu.VMEM((total, deep), bf16),
             pltpu.VMEM((total, width), f32),
             pltpu.VMEM((outs, width), bf16),
@@ -767,7 +822,7 @@
             pltpu.VMEM(anchors.shape, jnp.int32),
             pltpu.VMEM(blend_weight.shape, jnp.int32),
             pltpu.VMEM((PATCH * PATCH, 8, total), f32),
-            pltpu.VMEM((PATCH * PATCH, total, spread), bf16),
+            pltpu.VMEM((PATCH, total, spread), bf16),
             pltpu.VMEM((3, 8, 128), f32),
             pltpu.VMEM((8, 128), f32),
             pltpu.VMEM((8, 128), f32),
@@ -775,15 +830,15 @@
             pltpu.VMEM((total, 128), f32),
             pltpu.VMEM((outs + 16, total), f32),
             pltpu.VMEM((2, outs, 128), f32),
+            pltpu.VMEM((PATCH * C, band), f32),
             pltpu.VMEM((PATCH * C, band), bf16),
-            pltpu.VMEM((PATCH * C, band), bf16),
-            pltpu.VMEM((PATCH * C, band), bf16),
+            pltpu.VMEM((PATCH * C, band), f32),
             pltpu.VMEM((PATCH * C, band), bf16),
             dma((6 + 2 * windows,)),
-            dma((1,)),
-            dma((4 * reach + 1,)),
-            dma((2 * (reach - 2) + 6,)),
-            dma((3 * (reach - 3) + 11,)),
+            dma((2,)),
+            dma((5 * reach - 1,)),
+            dma((2 * (reach - 2) + 3,)),
+            dma((3 * (reach - 3) + 12,)),
             dma((4,)),
             dma((4,)),
         ],

time: 43.8 us -> 43 us (0.982)
  Pallas kernels: 43 us -> 42.2 us
    pallas_call x1, Pallas kernels: 43 us -> 42.2 us  [shards(): pl.pallas_call(functools.partial(block_kernel, n), out_shape=pltpu.VMEM((...]
where the time goes in v4:
time: 43 us; the launch traced here: 42.9 us
  Pallas kernels  42.2 us (98%)
  local copies, waits for them, and re-layouts  0.66 us (2%)
    pallas_call x1, Pallas kernels, shards(): pl.pallas_call(functools.partial(block_kernel, n), out_shape=pltpu.VMEM((...  42.2 us

profile of v4, /device:TPU:8, one launch (start us, length us, event | category | flops | bytes accessed | tf_op | source)
XLA Modules:
  0.0 42.9 jit_solution(9745340655594748863)
XLA Ops:
  0.0 42.2 %shard_map.82 = f32[256,64]{1,0:T(8,128)S(1)} custom-call(bf16[2,256,4608]{2,1,0:T(8,128)(2,1)} %qkv_hbm.1, bf16[2,128,3072]{2,1,0:T(8,128)(2,1)} %txt_hbm.1, bf16[512,3072]{1,0:T(8,128)(2,1)} %bitcast.4, bf16[96,3072]{1,0:T(8,128)(2,1)} %wp_hbm.1, bf16[64,3072]{1,0:T(8,128)(2,1)} %bitcast.5, f32[3,3072]{1,0:T(4,128)} %mod_hbm.1, s32[2,2]{1,0:T(2,128)} %anchors_hbm.1, ...), custom_call_target="tpu_custom_call" | custom-call | tf_op jit(solution)/shard_map/pallas_call | solution.py:802
  42.2 0.7 %copy.10 = f32[16,16,64]{2,1,0:T(8,128)} copy(f32[16,16,64]{2,1,0:T(8,128)S(1)} %bitcast.3) | data formatting | bytes 131072

commit v5 on v4

--- a/solution.py
+++ b/solution.py
@@ -245,13 +245,17 @@
         there = ring_recv.at[slots.index((d, piece))]
         return remote(ref, ref, sent.at[d // reach], there, backward if way else onward)
 
+    def final_cut(way, side_of):
+        col = column(way, group, 2)
+        return col + side_of * half, half
+
     def final_ring(way, side_of, which_core):
-        ref = region(source(way, last), which_core, *cut(way, group, (2, side_of)))
+        ref = region(source(way, last), which_core, *final_cut(way, side_of))
         there = ring_recv.at[len(slots) + side_of]
         return remote(ref, ref, sent.at[1], there, backward if way else onward)
 
     def final_part(way, side_of):
-        col, cols = cut(way, group, (2, side_of))
+        col, cols = final_cut(way, side_of)
         row = pl.multiple_of(source(way, reach) * deep, 16)
         ref = weights.at[pl.ds(row, deep), pl.ds(pl.multiple_of(col, 128), cols)]
         there = part_recv.at[len(part_groups) + side_of]
@@ -723,10 +727,9 @@
     only(0, some(end, 0))
     serve(*slots[tail + 1])
     take_across(1)
-    only(1, some(end, 0), some(serve_final, 0), some(close, 0), some(serve_final, 1))
+    only(1, some(end, 0), some(serve_final, 0), some(close, 0), some(serve_final, 1), some(close, 1))
     end(1)
-    only(0, some(take_final, 0), some(close, 0), some(take_final, 1))
-    close(1)
+    only(0, some(take_final, 0), some(close, 0), some(take_final, 1), some(close, 1))
 
     flat_one = vel[outs : outs + 1, :] * (1.0 / width)
     flat_two = jnp.sum(sum_two[...].T, axis=0, keepdims=True) * (1.0 / width)
@@ -879,7 +882,7 @@
             and n % 4 == 0
             and n >= 16
             and rows % 16 == 0
-            and width % 1536 == 0
+            and width % 3072 == 0
         )
         if ringed:
             return shards(n, *args)

time: 43 us -> 42.9 us (level)
  no operation moved by 1% of the time
where the time goes in v5:
time: 42.9 us; the launch traced here: 42.8 us
  Pallas kernels  42.1 us (98%)
  local copies, waits for them, and re-layouts  0.66 us (2%)
    pallas_call x1, Pallas kernels, shards(): pl.pallas_call(functools.partial(block_kernel, n), out_shape=pltpu.VMEM((...  42.1 us

profile of v5, /device:TPU:8, one launch (start us, length us, event | category | flops | bytes accessed | tf_op | source)
XLA Modules:
  0.0 42.8 jit_solution(1431223733225886382)
XLA Ops:
  0.0 42.1 %shard_map.82 = f32[256,64]{1,0:T(8,128)S(1)} custom-call(bf16[2,256,4608]{2,1,0:T(8,128)(2,1)} %qkv_hbm.1, bf16[2,128,3072]{2,1,0:T(8,128)(2,1)} %txt_hbm.1, bf16[512,3072]{1,0:T(8,128)(2,1)} %bitcast.4, bf16[96,3072]{1,0:T(8,128)(2,1)} %wp_hbm.1, bf16[64,3072]{1,0:T(8,128)(2,1)} %bitcast.5, f32[3,3072]{1,0:T(4,128)} %mod_hbm.1, s32[2,2]{1,0:T(2,128)} %anchors_hbm.1, ...), custom_call_target="tpu_custom_call" | custom-call | tf_op jit(solution)/shard_map/pallas_call | solution.py:805
  42.1 0.7 %copy.10 = f32[16,16,64]{2,1,0:T(8,128)} copy(f32[16,16,64]{2,1,0:T(8,128)S(1)} %bitcast.3) | data formatting | bytes 131072

commit v6 on v5

--- a/solution.py
+++ b/solution.py
@@ -247,7 +247,7 @@
 
     def final_cut(way, side_of):
         col = column(way, group, 2)
-        return col + side_of * half, half
+        return (col + 3 * half // 2, half // 2) if side_of else (col, 3 * half // 2)
 
     def final_ring(way, side_of, which_core):
         ref = region(source(way, last), which_core, *final_cut(way, side_of))
@@ -417,8 +417,8 @@
         )
         acc[:, at] += mod[0:1, at] * term
 
-    def finalize(cols, far=None, first=False):
-        spans = [pl.ds(pl.multiple_of(col, 128), half) for col in cols]
+    def finalize(cols, far=None, first=False, wide=half):
+        spans = [pl.ds(pl.multiple_of(col, 128), wide) for col in cols]
         held = [source(0, reach)] if far is None else [toward(far, last), source(0, reach)]
         term = jnp.dot(
             left_last[...] if far is None else left_close[far],
@@ -428,11 +428,11 @@
         lanes = centre.shape[1]
         pieces = []
         for i, at in enumerate(spans):
-            residual = acc[:, at] + mod[0:1, at] * term[:, i * half : (i + 1) * half]
+            residual = acc[:, at] + mod[0:1, at] * term[:, i * wide : (i + 1) * wide]
             if first and i == 0:
-                mean = jnp.sum(residual, axis=-1, keepdims=True) * (1.0 / half)
+                mean = jnp.sum(residual, axis=-1, keepdims=True) * (1.0 / wide)
                 centre[...] = jnp.broadcast_to(mean, centre.shape)
-            pieces += [residual[:, k : k + lanes] - centre[...] for k in range(0, half, lanes)]
+            pieces += [residual[:, k : k + lanes] - centre[...] for k in range(0, wide, lanes)]
         two = functools.reduce(lambda a, b: a + b, [x * x for x in pieces])
         sum_two[...] = two if first else sum_two[...] + two
         moved = jnp.concatenate(pieces, axis=1).astype(jnp.bfloat16)
@@ -624,12 +624,12 @@
                     final_ring(way, side_of, which_core).start()
 
     def serve_final(side_of):
-        arrived(ring_recv.at[len(slots) + side_of], 4)
+        arrived(ring_recv.at[len(slots) + side_of], 2 if side_of else 6)
         for way in range(2):
             final_part(way, side_of).start()
 
     def take_final(side_of):
-        arrived(part_recv.at[len(part_groups) + side_of], 4)
+        arrived(part_recv.at[len(part_groups) + side_of], 2 if side_of else 6)
 
     def serve_across(j):
         held = across_groups[j]
@@ -677,7 +677,8 @@
             finalize([t * unit, t * unit + half], far, first=t == 0)
 
     def close(side_of):
-        finalize([t * unit + side_of * half for t in (2, 3)])
+        start, wide = (3 * half // 2, half // 2) if side_of else (0, 3 * half // 2)
+        finalize([t * unit + start for t in (2, 3)], wide=wide)
 
     across_done = [0]
 

time: 42.9 us -> 42.8 us (level)
  no operation moved by 1% of the time
where the time goes in v6:
time: 42.8 us; the launch traced here: 42.7 us
  Pallas kernels  42 us (98%)
  local copies, waits for them, and re-layouts  0.66 us (2%)
    pallas_call x1, Pallas kernels, shards(): pl.pallas_call(functools.partial(block_kernel, n), out_shape=pltpu.VMEM((...  42 us

profile of v6, /device:TPU:8, one launch (start us, length us, event | category | flops | bytes accessed | tf_op | source)
XLA Modules:
  0.0 42.7 jit_solution(578049986658365038)
XLA Ops:
  0.0 42.0 %shard_map.82 = f32[256,64]{1,0:T(8,128)S(1)} custom-call(bf16[2,256,4608]{2,1,0:T(8,128)(2,1)} %qkv_hbm.1, bf16[2,128,3072]{2,1,0:T(8,128)(2,1)} %txt_hbm.1, bf16[512,3072]{1,0:T(8,128)(2,1)} %bitcast.4, bf16[96,3072]{1,0:T(8,128)(2,1)} %wp_hbm.1, bf16[64,3072]{1,0:T(8,128)(2,1)} %bitcast.5, f32[3,3072]{1,0:T(4,128)} %mod_hbm.1, s32[2,2]{1,0:T(2,128)} %anchors_hbm.1, ...), custom_call_target="tpu_custom_call" | custom-call | tf_op jit(solution)/shard_map/pallas_call | solution.py:806
  42.0 0.7 %copy.10 = f32[16,16,64]{2,1,0:T(8,128)} copy(f32[16,16,64]{2,1,0:T(8,128)S(1)} %bitcast.3) | data formatting | bytes 131072
